TPU v7x, 512 devices: a whole 4x8x8 slice. The times are simulated.
512 devices in a mesh: dp: 64 (over x, z, core), mp: 8 (over y).
Axes of the slice: x: 4, y: 8, z: 8, core: 2. Of those that a mesh axis runs over, the one named last changes fastest.
Arguments:
- inputs: bfloat16 [32768, 3968], P('dp', 'mp'), may hold values from -6 to 6
- grad_out: bfloat16 [32768, 2048], P('dp', 'mp'), may hold values from -0.25 to 0.25
- error: bfloat16 [131072, 3968], P(('dp', 'mp')), may hold values from -6 to 6
- q_prev: float32 [3968, 64], P('mp'), may hold values from -0.09375 to 0.09375
Outputs:
- new_error: bfloat16 [131072, 3968], P(('dp', 'mp'))
- p_basis: float32 [2048, 64], P('mp')
- q_factor: float32 [3968, 64], P('mp')
All inputs are finite; a program needn't handle non-finite values.
Results may differ from a plain program's by a relative error of at most 0.0065.
Values may be sent and summed in bfloat16 or wider, within the bound.
No kernel may reach another device: no remote copies, remote signals or barrier semaphores. Data moves between devices by JAX's collectives and lax.ppermute only.
A program may use at most 64 MiB of HBM per device.

v0:
```python
import jax
import jax.numpy as jnp
from jax import lax
from jax.sharding import Mesh
from jax.sharding import PartitionSpec as P

DP = ("dp_0", "dp_1", "dp_2")
DP_MP = ("dp_0", "dp_1", "dp_2", "mp")


def in_order(pieces, dim):
    pieces = jnp.moveaxis(pieces, 0, dim)
    shape = pieces.shape
    return pieces.reshape(*shape[:dim], shape[dim] * shape[dim + 1], *shape[dim + 2 :])


def sent_to_all(shard, axis):
    copies = jnp.broadcast_to(shard, (lax.axis_size(axis), *shard.shape))
    return lax.all_to_all(copies, axis, split_axis=0, concat_axis=0, tiled=True)


def gathered_copies(shard, axis, dim):
    return in_order(sent_to_all(shard, axis), dim)


def rows_for(lines, size):
    spare = -lines.shape[0] % size
    if not spare:
        return lines
    return jnp.concatenate([lines, jnp.zeros((spare, *lines.shape[1:]), lines.dtype)])


def cut_along(shard, dim, size):
    before, after = (shard.shape[:dim], shard.shape[dim + 1 :])
    return jnp.moveaxis(shard.reshape(*before, size, -1, *after), dim, 0)


def summed_on_arrival(shard, axis, dim):
    size = lax.axis_size(axis)
    pieces = lax.all_to_all(cut_along(shard, dim, size), axis, 0, 0, tiled=True)
    return jnp.sum(pieces, axis=0)


def sum_by_parts(shard, axes):
    lines = shard.reshape(-1, shard.shape[-1])
    padded = rows_for(lines, lax.axis_size(axes))
    whole = gathered_copies(summed_on_arrival(padded, axes, 0), axes, 0)
    return lax.slice_in_dim(whole, 0, len(lines)).reshape(shard.shape)


def taken_together(shard, axis):
    return sent_to_all(shard, axis).sum(axis=0)


def sum_by_axis(shard, axes, dim):
    far, near = axes
    pieces = cut_along(shard, dim, lax.axis_size(far))
    nearer = summed_on_arrival(pieces, near, dim + 1)
    arrived = lax.all_to_all(nearer, far, split_axis=0, concat_axis=0, tiled=True)
    return arrived.sum(axis=0)


def gathered_by_axis(shard, axes, dim):
    far, near = axes
    pieces = sent_to_all(sent_to_all(shard, far), near)
    return in_order(pieces.swapaxes(0, 1).reshape(-1, *shard.shape), dim)


def sum_by_parts_2(shard, axes):
    lines = shard.reshape(-1)
    own = sum_by_axis(rows_for(lines, lax.axis_size(axes[0]) * lax.axis_size(axes[1])), axes, 0)
    whole = gathered_by_axis(own, axes, 0)
    return whole[: len(lines)].reshape(shard.shape)


def per_device(inputs, grad_out, error, q_prev):
    highest = lax.Precision.HIGHEST
    replicas = lax.axis_size(DP)
    shards = lax.axis_size("mp")
    own_rows = grad_out.shape[1]
    own_cols = q_prev.shape[0]
    rank = q_prev.shape[1]
    q_full = gathered_copies(q_prev, "mp", 0)
    prod = lax.dot_general(
        grad_out,
        lax.all_gather(inputs, "mp", axis=1, tiled=True),
        (((0,), (0,)), ((), ())),
        preferred_element_type=jnp.float32,
    )
    merged = prod + error.astype(jnp.float32)
    local_p = jnp.dot(merged, q_full, precision=highest)
    factor = sum_by_parts(local_p, DP) / replicas
    gram = taken_together(jnp.dot(factor.T, factor, precision=highest), "mp")
    ridge = 0.01 * jnp.trace(gram) / rank + 1e-06
    gram = gram + ridge * jnp.eye(rank, dtype=jnp.float32)
    lower = jnp.linalg.cholesky(gram)
    p_hat = jax.scipy.linalg.solve_triangular(lower, factor.T, lower=True).T
    q_term = lax.dot_general(merged, p_hat, (((0,), (0,)), ((), ())), precision=highest)
    q_whole = sum_by_parts_2(q_term, (("dp_0", "dp_1"), ("dp_2", "mp"))) / replicas
    q_own = lax.dynamic_slice_in_dim(q_whole, lax.axis_index("mp") * own_cols, own_cols, 0)
    approx = jnp.dot(p_hat, q_whole.T, precision=highest)
    new_error = (merged - approx).astype(jnp.bfloat16)
    scale = jnp.sqrt(jnp.float32(own_rows * shards))
    return (new_error, p_hat * scale, q_own)


def solution(mesh):
    finer = Mesh(mesh.devices.reshape(4, 8, 2, mesh.shape["mp"]), ("dp_0", "dp_1", "dp_2", "mp"))
    in_specs = (P(DP, "mp"), P(DP, "mp"), P(DP_MP, None), P("mp", None))
    out_specs = (P(DP_MP, None), P("mp", None), P("mp", None))
    return jax.shard_map(
        per_device, mesh=finer, in_specs=in_specs, out_specs=out_specs, check_vma=False
    )
```

profile of v0, /device:TPU:1, one launch (start us, length us, event | category | flops | bytes accessed | tf_op | source)
XLA Modules:
  0.0 283.6 jit_solution(16322628270597437765)
XLA Ops:
  7.9 1.0 broadcast_in_dim.21
  8.9 38.5 %all_to_all.48 = f32[8,496,64]{1,2,0:T(8,128)S(1)} all-to-all(f32[8,496,64]{1,2,0:T(8,128)S(1)} %broadcast_in_dim.21), channel_id=1, replica_groups=mesh['dp_0'=4,'dp_1'=8,'dp_2'=2,'mp'=8] {'mp'}, dimensions={0} | all-to-all | bytes 2031616 | tf_op jit(solution)/shard_map/all_to_all | solution.py:19
  48.7 32.8 %all-gather.2.cloned.1.call-done = bf16[512,3968]{0,1:T(8,128)(2,1)} async-done(((bf16[512,496]{0,1:T(8,128)(2,1)}), bf16[512,3968]{0,1:T(8,128)(2,1)}) %all-gather.2.cloned.1.call-update) | async-done | bytes 4063248 | tf_op jit(solution)/shard_map/all_gather | solution.py:86
  81.5 6.0 %convolution_add_fusion = f32[256,3968]{1,0:T(8,128)} fusion(bf16[512,256]{1,0:T(8,128)(2,1)S(1)} %copy-done, bf16[512,3968]{0,1:T(8,128)(2,1)} %all-gather.2.cloned.1.call-done, bf16[256,3968]{1,0:T(8,128)(2,1)} %param.6), kind=kOutput, calls=%fused_computation.1 | convolution fusion | flops 1042219008 | bytes 10420224 | tf_op jit(solution)/shard_map/dot_general | solution.py:84
  87.5 5.3 %dot_general.18 = f32[64,4,3968]{2,1,0:T(4,128)} reshape(f32[256,3968]{1,0:T(8,128)} %convolution_add_fusion) | data formatting | bytes 8126464 | tf_op jit(solution)/shard_map/dot_general | solution.py:91
  92.8 5.6 %fusion.1 = f32[64,4,64]{2,0,1:T(8,128)S(1)} fusion(f32[3968,64,1]{0,1,2:T(8,128)S(1)} %reshape.34, f32[64,4,3968]{2,1,0:T(4,128)} %dot_general.18), kind=kOutput, calls=%fused_computation.3 | convolution fusion | flops 780140544 | bytes 5144576 | tf_op jit(solution)/shard_map/dot_general | solution.py:91
  98.7 23.4 %all_to_all.49 = f32[64,1,256]{2,1,0:T(1,128)S(1)} all-to-all(f32[64,1,256]{2,1,0:T(1,128)S(1)} %reshape.37), channel_id=1, replica_groups=mesh['dp_0'=4,'dp_1'=8,'dp_2'=2,'mp'=8] {'dp_0','dp_1','dp_2'}, dimensions={0} | all-to-all | bytes 131072 | tf_op jit(solution)/shard_map/all_to_all | solution.py:40
  123.8 13.6 %all_to_all.50 = f32[64,1,256]{2,1,0:T(1,128)S(1)} all-to-all(f32[64,1,256]{2,1,0:T(1,128)S(1)} %reshape.39), channel_id=1, replica_groups=mesh['dp_0'=4,'dp_1'=8,'dp_2'=2,'mp'=8] {'dp_0','dp_1','dp_2'}, dimensions={0} | all-to-all | bytes 131072 | tf_op jit(solution)/shard_map/all_to_all | solution.py:19
  138.7 0.8 reshape.41
  139.6 4.3 %all-to-all-start.3 = ((f32[8,1,4096]{2,1,0:T(1,128)}), f32[8,1,4096]{2,1,0:T(1,128)S(1)}, u32[]{:S(2)}, u32[]{:S(2)}) async-start(f32[8,1,4096]{2,1,0:T(1,128)} %reshape.41), calls=%async_computation.3 | async-start | bytes 262144 | tf_op jit(solution)/shard_map/all_to_all | solution.py:19
  143.9 7.8 %all-to-all-done.3 = f32[8,1,4096]{2,1,0:T(1,128)S(1)} async-done(((f32[8,1,4096]{2,1,0:T(1,128)}), f32[8,1,4096]{2,1,0:T(1,128)S(1)}, u32[]{:S(2)}, u32[]{:S(2)}) %all-to-all-start.3) | async-done | bytes 131104 | tf_op jit(solution)/shard_map/all_to_all | solution.py:19
  151.7 1.0 reduce.9
  154.2 5.8 %cholesky.17 = f32[64,64]{1,0:T(8,128)S(1)} custom-call(f32[64,64]{1,0:T(8,128)S(1)} %fusion.7), custom_call_target="Cholesky" | custom-call | tf_op jit(solution)/shard_map/jit(cholesky)/cholesky | solution.py:96
  161.4 4.9 %custom-call.7 = f32[1,64,64]{1,2,0:T(8,128)S(1)} custom-call(f32[1,64,64]{2,1,0:T(8,128)S(1)} %fusion.3), custom_call_target="InvertDiagBlocksLowerTriangular" | custom-call | tf_op jit(solution)/shard_map/jit(_solve_triangular)/triangular_solve | solution.py:97
  166.6 8.6 %fusion.8 = f32[3968,64]{1,0:T(8,128)S(1)} fusion(f32[256,3968]{1,0:T(8,128)} %convolution_add_fusion, f32[64,256]{1,0:T(8,128)S(1)} %fusion.4), kind=kOutput, calls=%fused_computation.24 | convolution fusion | flops 780140544 | bytes 5144576 | tf_op jit(solution)/shard_map/dot_general | solution.py:98
  175.2 1.0 reshape_reshape_reshape.4
  176.9 30.7 %all_to_all.51 = f32[16,32,496]{2,1,0:T(8,128)S(1)} all-to-all(f32[16,32,496]{2,1,0:T(8,128)S(1)} %copy.41), channel_id=1, replica_groups=mesh['dp_0'=4,'dp_1'=8,'dp_2'=2,'mp'=8] {'dp_2','mp'}, dimensions={0} | all-to-all | bytes 2031616 | tf_op jit(solution)/shard_map/all_to_all | solution.py:40
  207.7 11.8 %all_to_all.52 = f32[32,1,496]{2,1,0:T(1,128)S(1)} all-to-all(f32[32,1,496]{2,1,0:T(1,128)S(1)} %all_to_all.35), channel_id=1, replica_groups=mesh['dp_0'=4,'dp_1'=8,'dp_2'=2,'mp'=8] {'dp_0','dp_1'}, dimensions={0} | all-to-all | bytes 126976 | tf_op jit(solution)/shard_map/all_to_all | solution.py:59
  219.6 12.1 %all_to_all.53 = f32[32,1,496]{2,1,0:T(1,128)S(1)} all-to-all(f32[32,1,496]{2,1,0:T(1,128)S(1)} %broadcast_in_dim.25), channel_id=1, replica_groups=mesh['dp_0'=4,'dp_1'=8,'dp_2'=2,'mp'=8] {'dp_0','dp_1'}, dimensions={0} | all-to-all | bytes 126976 | tf_op jit(solution)/shard_map/all_to_all | solution.py:19
  231.7 1.1 broadcast_in_dim.26
  232.8 8.0 %all-to-all-start.7 = ((f32[16,32,496]{2,1,0:T(8,128)}), f32[16,32,496]{2,1,0:T(8,128)S(1)}, u32[]{:S(2)}, u32[]{:S(2)}) async-start(f32[16,32,496]{2,1,0:T(8,128)} %broadcast_in_dim.26), calls=%async_computation.7 | async-start | bytes 2097152 | tf_op jit(solution)/shard_map/all_to_all | solution.py:19
  241.4 26.0 %all-to-all-done.7 = f32[16,32,496]{2,1,0:T(8,128)S(1)} async-done(((f32[16,32,496]{2,1,0:T(8,128)}), f32[16,32,496]{2,1,0:T(8,128)S(1)}, u32[]{:S(2)}, u32[]{:S(2)}) %all-to-all-start.7) | async-done | bytes 1015840 | tf_op jit(solution)/shard_map/all_to_all | solution.py:19
  268.2 1.2 div.38
  269.4 6.6 %fusion = bf16[256,3968]{1,0:T(8,128)(2,1)} fusion(f32[256,3968]{1,0:T(8,128)} %convolution_add_fusion, f32[64,256]{1,0:T(8,128)S(1)} %fusion.4, f32[3968,64]{1,0:T(8,128)S(1)} %div.38), kind=kOutput, calls=%fused_computation.2 | convolution fusion | flops 782172160 | bytes 7176192 | tf_op jit(solution)/shard_map/dot_general | solution.py:101
  (40 shorter events, 10.7 us)
Async XLA Ops:
  7.2 74.3 %copy-start = (bf16[512,256]{1,0:T(8,128)(2,1)S(1)}, bf16[512,256]{1,0:T(8,128)(2,1)}, u32[]{:S(2)}) copy-start(bf16[512,256]{1,0:T(8,128)(2,1)} %param.5) | copy-start | bytes 786436
  7.2 74.3 %all-gather.2.cloned.1.call-start = ((), (), s32[]{:S(2)}) async-start(), calls=%async_computation.8 | async-start | bytes 4571136 | tf_op jit(solution)/shard_map/all_gather | solution.py:86
  139.6 12.1 %all-to-all-start.3 = ((f32[8,1,4096]{2,1,0:T(1,128)}), f32[8,1,4096]{2,1,0:T(1,128)S(1)}, u32[]{:S(2)}, u32[]{:S(2)}) async-start(f32[8,1,4096]{2,1,0:T(1,128)} %reshape.41), calls=%async_computation.3 | async-start | bytes 262144 | tf_op jit(solution)/shard_map/all_to_all | solution.py:19
  232.8 34.6 %all-to-all-start.7 = ((f32[16,32,496]{2,1,0:T(8,128)}), f32[16,32,496]{2,1,0:T(8,128)S(1)}, u32[]{:S(2)}, u32[]{:S(2)}) async-start(f32[16,32,496]{2,1,0:T(8,128)} %broadcast_in_dim.26), calls=%async_computation.7 | async-start | bytes 2097152 | tf_op jit(solution)/shard_map/all_to_all | solution.py:19
Sparse Core Ops, SparseCore 0:
  10.1 71.3 all-gather.1
where the time goes:
time: 284 us
  blocking collectives  130 us (46%)
  waiting for transfers between devices  67.2 us (24%)
  matrix products  27.6 us (10%)
  other arithmetic  16.3 us (6%)
  local copies, waits for them, and re-layouts  15.2 us (5%)
  between operations  14.9 us (5%)
  starting transfers between devices  12.3 us (4%)
    all_to_all x3, blocking collectives, sent_to_all(): return lax.all_to_all(copies, axis, split_axis=0, concat_axis=0, tiled=True)  64.3 us
    all_to_all x2, blocking collectives, summed_on_arrival(): pieces = lax.all_to_all(cut_along(shard, dim, size), axis, 0, 0, tiled=True)  54.1 us
    all_to_all x2, waiting for transfers between devices, sent_to_all(): return lax.all_to_all(copies, axis, split_axis=0, concat_axis=0, tiled=True)  33.7 us
    all_gather x1, waiting for transfers between devices, per_device(): lax.all_gather(inputs, 'mp', axis=1, tiled=True)  32.8 us
    all_to_all x2, starting transfers between devices, sent_to_all(): return lax.all_to_all(copies, axis, split_axis=0, concat_axis=0, tiled=True)  12.2 us
    all_to_all x1, blocking collectives, sum_by_axis(): lax.all_to_all(nearer, far, split_axis=0, concat_axis=0, tiled=True)  11.8 us
    dot_general x1, matrix products, per_device(): lax.dot_general(merged, p_hat, (((0,), (0,)), ((), ())), precision=highest)  8.63 us
    dot_general x1, matrix products, per_device(): approx = jnp.dot(p_hat, q_whole.T, precision=highest)  6.6 us
  transfers between devices with their start and end apart: 3, of which 3 were waited for; matrix products, arithmetic and copies ran while one was open for 1% of the time, Pallas kernels for 0%

commit v1 on v0

v1 whole, which is shorter than its diff:
```python
import jax
import jax.numpy as jnp
from jax import lax
from jax.sharding import Mesh
from jax.sharding import PartitionSpec as P

DP = ("dp_0", "dp_1", "dp_2")
DP_MP = ("dp_0", "dp_1", "dp_2", "mp")
BF16 = jnp.bfloat16
F32 = jnp.float32
HIGHEST = lax.Precision.HIGHEST


def exchange(pieces, axes):
    return lax.all_to_all(pieces, axes, split_axis=0, concat_axis=0, tiled=True)


def sent_to_all(shard, axes):
    return exchange(jnp.broadcast_to(shard, (lax.axis_size(axes), *shard.shape)), axes)


def in_columns(blocks):
    return jnp.concatenate([blocks[i] for i in range(blocks.shape[0])], axis=1)


def nt(a, b, **kw):
    return lax.dot_general(a, b, (((1,), (1,)), ((), ())), preferred_element_type=F32, **kw)


def nn(a, b, **kw):
    return lax.dot_general(a, b, (((1,), (0,)), ((), ())), preferred_element_type=F32, **kw)


def two_parts(value):
    high = lax.reduce_precision(value, 8, 7)
    return high.astype(BF16), (value - high).astype(BF16)


def per_device(inputs, grad_out, error, q_prev):
    replicas = lax.axis_size(DP)
    shards = lax.axis_size("mp")
    tokens, cols = inputs.shape
    rows = grad_out.shape[1]
    rank = q_prev.shape[1]
    half = tokens // 2
    x_t = inputs.T
    q_t = q_prev.T

    q_high, q_low = two_parts(q_t)
    xq = nn(q_high, x_t) + nn(q_low, x_t)
    first = sent_to_all(jnp.concatenate([xq.astype(BF16), q_high], axis=1), "mp")
    xq_sum = jnp.sum(first[:, :, :tokens].astype(F32), axis=0)
    q_full = in_columns(first[:, :, tokens:])
    x_a, first_seen = lax.optimization_barrier((inputs[:half], first[0, 0, 0]))
    x_a = lax.all_gather(x_a, "mp", axis=1, tiled=True)

    p_part = nn(xq_sum.astype(BF16), grad_out) + nt(q_full, error)
    p_row = jnp.sum(exchange(p_part, DP), axis=0) / replicas
    p_t = sent_to_all(p_row, DP)

    p_b = p_t.astype(BF16)
    gram_part = nt(p_t, p_t, precision=HIGHEST)
    gram_high, gram_low = two_parts(gram_part)
    gp = nt(p_b, grad_out).astype(BF16)
    ep = nn(p_b, error).astype(BF16)
    same = jnp.concatenate([gp, gram_high, gram_low], axis=1)
    ep_parts = jnp.moveaxis(ep.reshape(rank, shards, cols), 1, 0)
    same_parts = jnp.broadcast_to(same, (shards, *same.shape))
    pieces = jnp.concatenate([same_parts, ep_parts], axis=2)
    second = exchange(pieces, "mp")
    total = jnp.sum(second.astype(F32), axis=0)
    x_b, second_seen = lax.optimization_barrier((inputs[half:], second[0, 0, 0]))
    x_b = lax.all_gather(x_b, "mp", axis=1, tiled=True)
    gp_sum = total[:, :tokens]
    gram = total[:, tokens : tokens + rank] + total[:, tokens + rank : tokens + 2 * rank]
    ep_sum = total[:, tokens + 2 * rank :]

    q_part = nt(gp_sum.astype(BF16), x_t) + ep_sum
    q_row = jnp.sum(exchange(q_part, DP), axis=0) / replicas
    mixed = sent_to_all(q_row, DP)

    ridge = 0.01 * jnp.trace(gram) / rank + 1e-06
    eye = jnp.eye(rank, dtype=F32)
    lower = jnp.linalg.cholesky(gram + ridge * eye, symmetrize_input=False)
    inverse = jax.scipy.linalg.solve_triangular(lower, eye, lower=True)
    p_hat = nn(inverse, p_t, precision=HIGHEST)
    q_own = nn(inverse, mixed, precision=HIGHEST)

    q_whole = in_columns(sent_to_all(q_own.astype(BF16), "mp"))
    tn = (((0,), (0,)), ((), ()))
    merged = (
        lax.dot_general(grad_out[:half], x_a, tn, preferred_element_type=F32)
        + lax.dot_general(grad_out[half:], x_b, tn, preferred_element_type=F32)
        + error.astype(F32)
    )
    approx = lax.dot_general(p_hat.astype(BF16), q_whole, tn, preferred_element_type=F32)
    new_error = (merged - approx).astype(BF16)
    scale = jnp.sqrt(F32(rows * shards))
    return (new_error, (p_hat * scale).T, q_own.T)


def solution(mesh):
    finer = Mesh(mesh.devices.reshape(4, 8, 2, mesh.shape["mp"]), ("dp_0", "dp_1", "dp_2", "mp"))
    in_specs = (P(DP, "mp"), P(DP, "mp"), P(DP_MP, None), P("mp", None))
    out_specs = (P(DP_MP, None), P("mp", None), P("mp", None))
    return jax.shard_map(
        per_device, mesh=finer, in_specs=in_specs, out_specs=out_specs, check_vma=False
    )
```

time: 284 us -> 217 us (0.76)
  blocking collectives: 130 us -> 43.1 us
  starting transfers between devices: 12.3 us -> 28.2 us
  waiting for transfers between devices: 67.2 us -> 80.2 us
  matrix products: 27.6 us -> 20.6 us
  local copies, waits for them, and re-layouts: 15.2 us -> 10.2 us
    all_to_all x6 -> x2, blocking collectives: 130 us -> 43.1 us  [exchange(): return lax.all_to_all(pieces, axes, split_axis=0, concat_axis=0, tiled=True)]
    all_to_all x2 -> x5, waiting for transfers between devices: 33.7 us -> 79.4 us  [exchange(): return lax.all_to_all(pieces, axes, split_axis=0, concat_axis=0, tiled=True)]
    all_gather x1 -> x2, waiting for transfers between devices: 32.8 us -> 0.03 us  [the longest x1 0.02 us: per_device(): x_a = lax.all_gather(x_a, 'mp', axis=1, tiled=True)]
    all_to_all x2 -> x5, starting transfers between devices: 12.2 us -> 28.1 us  [exchange(): return lax.all_to_all(pieces, axes, split_axis=0, concat_axis=0, tiled=True)]
    dot_general x5 -> x13, matrix products: 27.3 us -> 20.4 us  [the longest x1 5.43 us: per_device(): lax.dot_general(grad_out[half:], x_b, tn, preferred_element_type=F32)]
    dot_general x2 -> x0, local copies, waits for them, and re-layouts: 5.37 us -> none  [per_device(): local_p = jnp.dot(merged, q_full, precision=highest)]
  transfers between devices with their start and end apart: 3 -> 7, of which waited for: 3 -> 5; matrix products, arithmetic and copies ran while one was open for 1% -> 19% of each run, Pallas kernels for 0% -> 0%
where the time goes in v1:
time: 217 us; the launch traced here: 216 us
  waiting for transfers between devices  80.2 us (37%)
  blocking collectives  43.1 us (20%)
  starting transfers between devices  28.2 us (13%)
  matrix products  20.6 us (9%)
  other arithmetic  18.5 us (9%)
  between operations  14.9 us (7%)
  local copies, waits for them, and re-layouts  10.2 us (5%)
    all_to_all x5, waiting for transfers between devices, exchange(): return lax.all_to_all(pieces, axes, split_axis=0, concat_axis=0, tiled=True)  79.4 us
    all_to_all x2, blocking collectives, exchange(): return lax.all_to_all(pieces, axes, split_axis=0, concat_axis=0, tiled=True)  43.1 us
    all_to_all x5, starting transfers between devices, exchange(): return lax.all_to_all(pieces, axes, split_axis=0, concat_axis=0, tiled=True)  28.1 us
    another operation x3, other arithmetic, per_device(): lower = jnp.linalg.cholesky(gram + ridge * eye, symmetrize_input=False)  6.52 us
    another operation x2, other arithmetic, per_device(): inverse = jax.scipy.linalg.solve_triangular(lower, eye, lower=True)  5.55 us
    dot_general x1, matrix products, per_device(): lax.dot_general(grad_out[half:], x_b, tn, preferred_element_type=F32)  5.43 us
    dot_general x6, matrix products, nn(): lax.dot_general(a, b, (((1,), (0,)), ((), ())), preferred_element_type=F3...  5.14 us
  transfers between devices with their start and end apart: 7, of which 5 were waited for; matrix products, arithmetic and copies ran while one was open for 19% of the time, Pallas kernels for 0%

profile of v1, /device:TPU:1, one launch (start us, length us, event | category | flops | bytes accessed | tf_op | source)
XLA Modules:
  0.0 215.6 jit_solution(7646437302904327524)
XLA Ops:
  8.1 1.2 fusion.26
  9.3 1.4 fusion.3
  11.8 7.6 %all-to-all-start = ((bf16[8,64,1008]{2,1,0:T(8,128)(2,1)}), bf16[8,64,1008]{2,1,0:T(8,128)(2,1)}, u32[]{:S(2)}, u32[]{:S(2)}) async-start(bf16[8,64,1008]{2,1,0:T(8,128)(2,1)} %broadcast_in_dim.21), calls=%async_computation | async-start | bytes 2097152 | tf_op jit(solution)/shard_map/all_to_all | solution.py:15
  20.4 25.9 %all-to-all-done = bf16[8,64,1008]{2,1,0:T(8,128)(2,1)} async-done(((bf16[8,64,1008]{2,1,0:T(8,128)(2,1)}), bf16[8,64,1008]{2,1,0:T(8,128)(2,1)}, u32[]{:S(2)}, u32[]{:S(2)}) %all-to-all-start) | async-done | bytes 1032224 | tf_op jit(solution)/shard_map/all_to_all | solution.py:15
  46.3 1.8 slice_bitcast_fusion.8
  48.1 1.3 concatenate.16
  51.5 29.5 %all_to_all.51 = f32[64,1,256]{2,1,0:T(1,128)S(1)} all-to-all(f32[64,1,256]{2,1,0:T(1,128)S(1)} %copy.11), channel_id=1, replica_groups=mesh['dp_0'=4,'dp_1'=8,'dp_2'=2,'mp'=8] {'dp_0','dp_1','dp_2'}, dimensions={0} | all-to-all | bytes 131072 | tf_op jit(solution)/shard_map/all_to_all | solution.py:15
  81.1 13.6 %all_to_all.52 = f32[64,1,256]{2,1,0:T(1,128)S(1)} all-to-all(f32[64,1,256]{2,1,0:T(1,128)S(1)} %broadcast_in_dim.22), channel_id=1, replica_groups=mesh['dp_0'=4,'dp_1'=8,'dp_2'=2,'mp'=8] {'dp_0','dp_1','dp_2'}, dimensions={0} | all-to-all | bytes 131072 | tf_op jit(solution)/shard_map/all_to_all | solution.py:15
  94.8 1.3 convolution_convert_fusion
  96.0 2.1 reshape.31
  100.0 4.3 %all-to-all-start.3 = ((bf16[8,64,1136]{2,1,0:T(8,128)(2,1)}), bf16[8,64,1136]{2,1,0:T(8,128)(2,1)}, u32[]{:S(2)}, u32[]{:S(2)}) async-start(bf16[8,64,1136]{2,1,0:T(8,128)(2,1)} %pad_maximum_fusion), calls=%async_computation.3 | async-start | bytes 2359296 | tf_op jit(solution)/shard_map/all_to_all | solution.py:15
  105.1 4.2 %fusion.10 = f32[256,3968]{1,0:T(8,128)} fusion(bf16[256,3968]{0,1:T(8,128)(2,1)} %all-gather.3.cloned.1.call-done, bf16[512,256]{1,0:T(8,128)(2,1)S(1)} %copy-done.2), kind=kOutput, calls=%fused_computation.25 | convolution fusion | flops 520093696 | bytes 6225920 | tf_op jit(solution)/shard_map/dot_general | solution.py:92
  109.3 34.8 %all-to-all-done.3 = bf16[8,64,1136]{2,1,0:T(8,128)(2,1)} async-done(((bf16[8,64,1136]{2,1,0:T(8,128)(2,1)}), bf16[8,64,1136]{2,1,0:T(8,128)(2,1)}, u32[]{:S(2)}, u32[]{:S(2)}) %all-to-all-start.3) | async-done | bytes 1163296 | tf_op jit(solution)/shard_map/all_to_all | solution.py:15
  144.1 1.5 convert_reduce_fusion
  146.7 4.7 %all-to-all-start.4 = ((f32[64,1,496]{2,1,0:T(1,128)}), f32[64,1,496]{2,1,0:T(1,128)S(1)}, u32[]{:S(2)}, u32[]{:S(2)}) async-start(f32[64,1,496]{2,1,0:T(1,128)} %copy.13), calls=%async_computation.4 | async-start | bytes 262144 | tf_op jit(solution)/shard_map/all_to_all | solution.py:15
  152.8 5.8 %cholesky.18 = f32[64,64]{1,0:T(8,128)S(1)} custom-call(f32[64,64]{1,0:T(8,128)S(1)} %select_add_fusion), custom_call_target="Cholesky" | custom-call | tf_op jit(solution)/shard_map/jit(cholesky)/cholesky | solution.py:84
  159.3 2.5 %all-to-all-done.4 = f32[64,1,496]{2,1,0:T(1,128)S(1)} async-done(((f32[64,1,496]{2,1,0:T(1,128)}), f32[64,1,496]{2,1,0:T(1,128)S(1)}, u32[]{:S(2)}, u32[]{:S(2)}) %all-to-all-start.4) | async-done | bytes 127008 | tf_op jit(solution)/shard_map/all_to_all | solution.py:15
  162.7 7.9 %all-to-all-start.5 = ((f32[64,1,496]{2,1,0:T(1,128)}), f32[64,1,496]{2,1,0:T(1,128)S(1)}, u32[]{:S(2)}, u32[]{:S(2)}) async-start(f32[64,1,496]{2,1,0:T(1,128)} %broadcast_in_dim.25), calls=%async_computation.5 | async-start | bytes 262144 | tf_op jit(solution)/shard_map/all_to_all | solution.py:15
  171.3 4.9 %custom-call.7 = f32[1,64,64]{1,2,0:T(8,128)S(1)} custom-call(f32[1,64,64]{2,1,0:T(8,128)S(1)} %fusion.19), custom_call_target="InvertDiagBlocksLowerTriangular" | custom-call | tf_op jit(solution)/shard_map/jit(_solve_triangular)/triangular_solve | solution.py:85
  176.4 4.5 %all-to-all-done.5 = f32[64,1,496]{2,1,0:T(1,128)S(1)} async-done(((f32[64,1,496]{2,1,0:T(1,128)}), f32[64,1,496]{2,1,0:T(1,128)S(1)}, u32[]{:S(2)}, u32[]{:S(2)}) %all-to-all-start.5) | async-done | bytes 127008 | tf_op jit(solution)/shard_map/all_to_all | solution.py:15
  182.7 3.6 %all-to-all-start.6 = ((bf16[8,64,496]{2,1,0:T(8,128)(2,1)}), bf16[8,64,496]{2,1,0:T(8,128)(2,1)S(1)}, u32[]{:S(2)}, u32[]{:S(2)}) async-start(bf16[8,64,496]{2,1,0:T(8,128)(2,1)} %broadcast_in_dim.26), calls=%async_computation.6 | async-start | bytes 1048576 | tf_op jit(solution)/shard_map/all_to_all | solution.py:15
  186.3 5.4 %fusion = f32[256,3968]{1,0:T(8,128)} fusion(f32[256,3968]{1,0:T(8,128)} %fusion.10, bf16[256,3968]{0,1:T(8,128)(2,1)} %all-gather.5.cloned.1.call-done, bf16[256,3968]{1,0:T(8,128)(2,1)S(1)} %copy-done, bf16[512,256]{1,0:T(8,128)(2,1)S(1)} %copy-done.2), kind=kOutput, calls=%fused_computation.2 | convolution fusion | flops 523141120 | bytes 12320768 | tf_op jit(solution)/shard_map/dot_general | solution.py:93
  192.6 11.7 %all-to-all-done.6 = bf16[8,64,496]{2,1,0:T(8,128)(2,1)S(1)} async-done(((bf16[8,64,496]{2,1,0:T(8,128)(2,1)}), bf16[8,64,496]{2,1,0:T(8,128)(2,1)S(1)}, u32[]{:S(2)}, u32[]{:S(2)}) %all-to-all-start.6) | async-done | bytes 507936 | tf_op jit(solution)/shard_map/all_to_all | solution.py:15
  204.6 4.2 %fusion.1 = bf16[256,3968]{1,0:T(8,128)(2,1)} fusion(f32[256,3968]{1,0:T(8,128)} %fusion, bf16[64,3968]{1,0:T(8,128)(2,1)S(1)} %concatenate.19, f32[64,256]{1,0:T(8,128)S(1)} %fusion.13), kind=kOutput, calls=%fused_computation.3 | convolution fusion | flops 132071424 | bytes 6668288 | tf_op jit(solution)/shard_map/dot_general | solution.py:96
  (46 shorter events, 15.0 us)
Async XLA Ops:
  9.3 10.2 %copy-start.1 = (bf16[512,496]{0,1:T(8,128)(2,1)S(1)}, bf16[512,496]{0,1:T(8,128)(2,1)}, u32[]{:S(2)}) copy-start(bf16[512,496]{0,1:T(8,128)(2,1)} %param.4) | copy-start | bytes 1523716
  11.8 34.5 %all-to-all-start = ((bf16[8,64,1008]{2,1,0:T(8,128)(2,1)}), bf16[8,64,1008]{2,1,0:T(8,128)(2,1)}, u32[]{:S(2)}, u32[]{:S(2)}) async-start(bf16[8,64,1008]{2,1,0:T(8,128)(2,1)} %broadcast_in_dim.21), calls=%async_computation | async-start | bytes 2097152 | tf_op jit(solution)/shard_map/all_to_all | solution.py:15
  19.5 31.0 %copy-start.2 = (bf16[512,256]{1,0:T(8,128)(2,1)S(1)}, bf16[512,256]{1,0:T(8,128)(2,1)}, u32[]{:S(2)}) copy-start(bf16[512,256]{1,0:T(8,128)(2,1)} %param.5) | copy-start | bytes 786436
  19.5 31.2 %copy-start = (bf16[256,3968]{1,0:T(8,128)(2,1)S(1)}, bf16[256,3968]{1,0:T(8,128)(2,1)}, u32[]{:S(2)}) copy-start(bf16[256,3968]{1,0:T(8,128)(2,1)} %param.6) | copy-start | bytes 6094852
  19.5 85.6 %all-gather.3.cloned.1.call-start = ((), (), s32[]{:S(2)}) async-start(), calls=%async_computation.7 | async-start | bytes 2285568 | tf_op jit(solution)/shard_map/all_gather | solution.py:55
  100.0 44.1 %all-to-all-start.3 = ((bf16[8,64,1136]{2,1,0:T(8,128)(2,1)}), bf16[8,64,1136]{2,1,0:T(8,128)(2,1)}, u32[]{:S(2)}, u32[]{:S(2)}) async-start(bf16[8,64,1136]{2,1,0:T(8,128)(2,1)} %pad_maximum_fusion), calls=%async_computation.3 | async-start | bytes 2359296 | tf_op jit(solution)/shard_map/all_to_all | solution.py:15
  104.3 82.0 %all-gather.5.cloned.1.call-start = ((), (), s32[]{:S(2)}) async-start(), calls=%async_computation.8 | async-start | bytes 2285568 | tf_op jit(solution)/shard_map/all_gather | solution.py:73
  146.7 15.2 %all-to-all-start.4 = ((f32[64,1,496]{2,1,0:T(1,128)}), f32[64,1,496]{2,1,0:T(1,128)S(1)}, u32[]{:S(2)}, u32[]{:S(2)}) async-start(f32[64,1,496]{2,1,0:T(1,128)} %copy.13), calls=%async_computation.4 | async-start | bytes 262144 | tf_op jit(solution)/shard_map/all_to_all | solution.py:15
  162.7 18.3 %all-to-all-start.5 = ((f32[64,1,496]{2,1,0:T(1,128)}), f32[64,1,496]{2,1,0:T(1,128)S(1)}, u32[]{:S(2)}, u32[]{:S(2)}) async-start(f32[64,1,496]{2,1,0:T(1,128)} %broadcast_in_dim.25), calls=%async_computation.5 | async-start | bytes 262144 | tf_op jit(solution)/shard_map/all_to_all | solution.py:15
  182.7 21.5 %all-to-all-start.6 = ((bf16[8,64,496]{2,1,0:T(8,128)(2,1)}), bf16[8,64,496]{2,1,0:T(8,128)(2,1)S(1)}, u32[]{:S(2)}, u32[]{:S(2)}) async-start(bf16[8,64,496]{2,1,0:T(8,128)(2,1)} %broadcast_in_dim.26), calls=%async_computation.6 | async-start | bytes 1048576 | tf_op jit(solution)/shard_map/all_to_all | solution.py:15
Sparse Core Ops, SparseCore 0:
  22.4 46.3 all-gather.2
  107.2 47.7 all-gather.4

commit v2 on v1

v2 whole, which is shorter than its diff:
```python
import jax
import jax.numpy as jnp
from jax import lax
from jax.experimental import pallas as pl
from jax.experimental.pallas import tpu as pltpu
from jax.sharding import Mesh
from jax.sharding import PartitionSpec as P

DP = ("dp_0", "dp_1", "dp_2")
DP_MP = ("dp_0", "dp_1", "dp_2", "mp")
BF16 = jnp.bfloat16
F32 = jnp.float32
HIGHEST = lax.Precision.HIGHEST


def exchange(pieces, axes):
    return lax.all_to_all(pieces, axes, split_axis=0, concat_axis=0, tiled=True)


def sent_to_all(shard, axes):
    return exchange(jnp.broadcast_to(shard, (lax.axis_size(axes), *shard.shape)), axes)


def nt(a, b, **kw):
    return lax.dot_general(a, b, (((1,), (1,)), ((), ())), preferred_element_type=F32, **kw)


def nn(a, b, **kw):
    return lax.dot_general(a, b, (((1,), (0,)), ((), ())), preferred_element_type=F32, **kw)


def local_call(body, name, outs, *args, flops=0):
    spec = pl.BlockSpec(memory_space=pltpu.VMEM)
    moved = sum(a.size * a.dtype.itemsize for a in (*args, *outs))
    return pl.pallas_call(
        body,
        name=name,
        out_shape=list(outs),
        in_specs=[spec] * len(args),
        out_specs=[spec] * len(outs),
        compiler_params=pltpu.CompilerParams(vmem_limit_bytes=16 * 1024 * 1024),
        cost_estimate=pl.CostEstimate(flops=flops, bytes_accessed=moved, transcendentals=0),
    )(*args)


def shaped(shape, dtype):
    return jax.ShapeDtypeStruct(shape, dtype)


def start_body(x_ref, q_ref, out_ref):
    tokens = x_ref.shape[1]
    q = q_ref[...]
    high = q.astype(BF16)
    low = (q - high.astype(F32)).astype(BF16)
    x = x_ref[...]
    out_ref[:, :tokens] = (nn(high, x) + nn(low, x)).astype(BF16)
    out_ref[:, tokens:] = high


def p_body(first_ref, g_ref, e_ref, x_ref, out_ref, x_half_ref):
    tokens = g_ref.shape[0]
    shards = first_ref.shape[0]
    x_half_ref[...] = x_ref[:, : x_half_ref.shape[1]]
    xq = first_ref[0, :, :tokens].astype(F32)
    for i in range(1, shards):
        xq = xq + first_ref[i, :, :tokens].astype(F32)
    q_full = jnp.concatenate([first_ref[i, :, tokens:] for i in range(shards)], axis=1)
    out_ref[...] = nn(xq.astype(BF16), g_ref[...]) + nt(q_full, e_ref[...])


def factors_body(p_ref, g_ref, e_ref, out_ref):
    tokens = g_ref.shape[0]
    shards, rank, width = out_ref.shape
    cols = width - tokens - 2 * rank
    p = p_ref[...]
    p_b = p.astype(BF16)
    gram = nt(p, p, precision=HIGHEST)
    high = gram.astype(BF16)
    low = (gram - high.astype(F32)).astype(BF16)
    gp = nt(p_b, g_ref[...]).astype(BF16)
    ep = nn(p_b, e_ref[...]).astype(BF16)
    both = jnp.concatenate([high, low], axis=1)
    for i in range(shards):
        out_ref[i, :, :tokens] = gp
        out_ref[i, :, tokens : tokens + 2 * rank] = both
        out_ref[i, :, tokens + 2 * rank :] = ep[:, i * cols : (i + 1) * cols]


def q_body(second_ref, x_ref, out_ref, gram_ref, x_half_ref):
    tokens = x_ref.shape[1]
    rank = out_ref.shape[0]
    half = x_half_ref.shape[1]
    x_half_ref[...] = x_ref[:, half:]
    total = second_ref[0].astype(F32)
    for i in range(1, second_ref.shape[0]):
        total = total + second_ref[i].astype(F32)
    both = total[:, tokens : tokens + 2 * rank]
    gram_ref[...] = both[:, :rank] + both[:, rank:]
    out_ref[...] = nt(total[:, :tokens].astype(BF16), x_ref[...]) + total[:, tokens + 2 * rank :]


def inverse_body(gram_ref, out_ref):
    rank = gram_ref.shape[0]
    row = lax.broadcasted_iota(jnp.int32, (rank, rank), 0)
    col = lax.broadcasted_iota(jnp.int32, (rank, rank), 1)
    eye = (row == col).astype(F32)
    gram = gram_ref[...]
    trace = jnp.sum(jnp.sum(gram * eye, axis=1, keepdims=True), axis=0, keepdims=True)
    ridge = 0.01 * trace / rank + 1e-06
    work = jnp.concatenate([gram + ridge * eye, eye], axis=1)
    below = lax.broadcasted_iota(jnp.int32, (rank, 2 * rank), 0)
    done = []
    for k in range(0, rank, 2):
        first, second = work[k : k + 1, :], work[k + 1 : k + 2, :]
        left, right = work[:, k : k + 1], work[:, k + 1 : k + 2]
        root = lax.rsqrt(first[:, k : k + 1])
        first, left = first * root, left * root
        cross = first[:, k + 1 : k + 2]
        root = lax.rsqrt(second[:, k + 1 : k + 2] - cross * cross)
        second = (second - cross * first) * root
        right = (right - cross * left) * root
        done.append(first[:, rank:])
        done.append(second[:, rank:])
        if k + 2 < rank:
            rest = below > k + 1
            work = work - (
                jnp.where(rest, left, 0.0) * first + jnp.where(rest, right, 0.0) * second
            )
    out_ref[...] = jnp.concatenate(done, axis=0)


def column_tiles(width, tile=512):
    return [(start, min(start + tile, width)) for start in range(0, width, tile)]


def merged_body(g_ref, e_ref, xa_ref, xb_ref, out_ref):
    half = xa_ref.shape[1]
    for lo, hi in column_tiles(e_ref.shape[1]):
        made = nt(g_ref[:, :half], xa_ref[lo:hi, :]) + nt(g_ref[:, half:], xb_ref[lo:hi, :])
        out_ref[:, lo:hi] = made + e_ref[:, lo:hi].astype(F32)


def residue_body(q_ref, p_ref, merged_ref, out_ref):
    shards = q_ref.shape[0]
    q_full = jnp.concatenate([q_ref[i] for i in range(shards)], axis=1)
    p_rows = p_ref[...]
    for lo, hi in column_tiles(merged_ref.shape[1]):
        approx = nn(p_rows, q_full[:, lo:hi])
        out_ref[:, lo:hi] = (merged_ref[:, lo:hi] - approx).astype(BF16)


def per_device(inputs, grad_out, error, q_prev):
    replicas = lax.axis_size(DP)
    shards = lax.axis_size("mp")
    tokens, cols = inputs.shape
    rows = grad_out.shape[1]
    rank = q_prev.shape[1]
    half = tokens // 2
    width = error.shape[1]
    x_t = inputs.T

    (packed,) = local_call(
        start_body,
        "start",
        [shaped((rank, tokens + cols), BF16)],
        x_t,
        q_prev.T,
        flops=4 * rank * tokens * cols,
    )
    first = lax.all_gather(packed, "mp")
    p_part, x_a = local_call(
        p_body,
        "p_part",
        [shaped((rank, rows), F32), shaped((cols, half), BF16)],
        first,
        grad_out,
        error,
        x_t,
        flops=2 * rank * rows * (tokens + width),
    )
    x_a = lax.all_gather(x_a, "mp", axis=0, tiled=True)
    p_row = jnp.sum(exchange(p_part, DP), axis=0) / replicas
    p_t = sent_to_all(p_row, DP)

    (pieces,) = local_call(
        factors_body,
        "factors",
        [shaped((shards, rank, tokens + 2 * rank + cols), BF16)],
        p_t,
        grad_out,
        error,
        flops=2 * rank * rows * (tokens + width),
    )
    second = exchange(pieces, "mp")
    q_part, gram, x_b = local_call(
        q_body,
        "q_part",
        [shaped((rank, cols), F32), shaped((rank, rank), F32), shaped((cols, half), BF16)],
        second,
        x_t,
        flops=2 * rank * cols * tokens,
    )
    x_b = lax.all_gather(x_b, "mp", axis=0, tiled=True)
    q_row = jnp.sum(exchange(q_part, DP), axis=0) / replicas
    mixed = sent_to_all(q_row, DP)

    (inverse,) = local_call(
        inverse_body, "inverse", [shaped((rank, rank), F32)], gram, flops=4 * rank**3
    )
    p_hat = nn(inverse, p_t, precision=HIGHEST)
    q_own = nn(inverse, mixed, precision=HIGHEST)

    q_parts = sent_to_all(q_own.astype(BF16), "mp")
    (merged,) = local_call(
        merged_body,
        "merged",
        [shaped((rows, width), F32)],
        grad_out.T,
        error,
        x_a,
        x_b,
        flops=2 * rows * width * tokens,
    )
    (new_error,) = local_call(
        residue_body,
        "residue",
        [shaped((rows, width), BF16)],
        q_parts,
        p_hat.astype(BF16).T,
        merged,
        flops=2 * rows * width * rank,
    )
    scale = jnp.sqrt(F32(rows * shards))
    return (new_error, (p_hat * scale).T, q_own.T)


def solution(mesh):
    finer = Mesh(mesh.devices.reshape(4, 8, 2, mesh.shape["mp"]), ("dp_0", "dp_1", "dp_2", "mp"))
    in_specs = (P(DP, "mp"), P(DP, "mp"), P(DP_MP, None), P("mp", None))
    out_specs = (P(DP_MP, None), P("mp", None), P("mp", None))
    return jax.shard_map(
        per_device, mesh=finer, in_specs=in_specs, out_specs=out_specs, check_vma=False
    )
```

time: 217 us -> 185 us (0.85)
  blocking collectives: 43.1 us -> 120 us
  waiting for transfers between devices: 80.2 us -> 15.3 us
  starting transfers between devices: 28.2 us -> 8.45 us
  matrix products: 20.6 us -> 1.75 us
  other arithmetic: 18.5 us -> 0.23 us
  Pallas kernels: 0 us -> 12.1 us
  local copies, waits for them, and re-layouts: 10.2 us -> 12.8 us
    all_to_all x5 -> x2, waiting for transfers between devices: 79.4 us -> 15.2 us  [exchange(): return lax.all_to_all(pieces, axes, split_axis=0, concat_axis=0, tiled=True)]
    all_to_all x2 -> x4, blocking collectives: 43.1 us -> 96 us  [exchange(): return lax.all_to_all(pieces, axes, split_axis=0, concat_axis=0, tiled=True)]
    all_gather x0 -> x1, blocking collectives: none -> 23.5 us  [per_device(): first = lax.all_gather(packed, 'mp')]
    all_to_all x5 -> x2, starting transfers between devices: 28.1 us -> 8.37 us  [exchange(): return lax.all_to_all(pieces, axes, split_axis=0, concat_axis=0, tiled=True)]
    dot_general x7 -> x0, matrix products: 15.3 us -> none  [the longest x1 5.43 us: per_device(): lax.dot_general(grad_out[half:], x_b, tn, preferred_element_type=F32)]
    another operation x5 -> x0, other arithmetic: 12.1 us -> none  [the longest x3 6.52 us: per_device(): lower = jnp.linalg.cholesky(gram + ridge * eye, symmetrize_input=False)]
    pallas_call x0 -> x7, Pallas kernels: none -> 12.1 us  [local_call(): pl.pallas_call(body, name=name, out_shape=list(outs), in_specs=[spec] * l...]
    unnamed x6 -> x22, local copies, waits for them, and re-layouts: 0.02 us -> 10.8 us
  transfers between devices with their start and end apart: 7 -> 4, of which waited for: 5 -> 2; matrix products, arithmetic and copies ran while one was open for 19% -> 2% of each run, Pallas kernels for 0% -> 5%
where the time goes in v2:
time: 185 us; the launch traced here: 184 us
  blocking collectives  120 us (65%)
  waiting for transfers between devices  15.3 us (8%)
  between operations  14.2 us (8%)
  local copies, waits for them, and re-layouts  12.8 us (7%)
  Pallas kernels  12.1 us (7%)
  starting transfers between devices  8.45 us (5%)
    all_to_all x4, blocking collectives, exchange(): return lax.all_to_all(pieces, axes, split_axis=0, concat_axis=0, tiled=True)  96 us
    all_gather x1, blocking collectives, per_device(): first = lax.all_gather(packed, 'mp')  23.5 us
    all_to_all x2, waiting for transfers between devices, exchange(): return lax.all_to_all(pieces, axes, split_axis=0, concat_axis=0, tiled=True)  15.2 us
    pallas_call x7, Pallas kernels, local_call(): pl.pallas_call(body, name=name, out_shape=list(outs), in_specs=[spec] * l...  12.1 us
    unnamed x22, local copies, waits for them, and re-layouts  10.8 us
    all_to_all x2, starting transfers between devices, exchange(): return lax.all_to_all(pieces, axes, split_axis=0, concat_axis=0, tiled=True)  8.37 us
  transfers between devices with their start and end apart: 4, of which 2 were waited for; matrix products, arithmetic and copies ran while one was open for 2% of the time, Pallas kernels for 5%

profile of v2, /device:TPU:1, one launch (start us, length us, event | category | flops | bytes accessed | tf_op | source)
XLA Modules:
  0.0 184.2 jit_solution(81017771897268433)
XLA Ops:
  7.2 1.0 copy-done.4
  8.3 0.9 copy-done.9
  9.4 23.5 %all-gather = bf16[512,1008]{1,0:T(8,128)(2,1)S(1)} all-gather(bf16[64,1008]{1,0:T(8,128)(2,1)S(1)} %start.1), channel_id=2, replica_groups=mesh['dp_0'=4,'dp_1'=8,'dp_2'=2,'mp'=8] {'mp'}, dimensions={0}, use_global_device_ids=true | all-gather | bytes 1161216 | tf_op jit(solution)/shard_map/all_gather | solution.py:170
  32.9 1.6 copy-done
  34.5 1.4 p_part.1
  36.0 29.3 %all_to_all.45 = f32[64,1,256]{2,1,0:T(1,128)S(1)} all-to-all(f32[64,1,256]{2,1,0:T(1,128)S(1)} %copy.13), channel_id=1, replica_groups=mesh['dp_0'=4,'dp_1'=8,'dp_2'=2,'mp'=8] {'dp_0','dp_1','dp_2'}, dimensions={0} | all-to-all | bytes 131072 | tf_op jit(solution)/shard_map/all_to_all | solution.py:17
  65.4 13.6 %all_to_all.46 = f32[64,1,256]{2,1,0:T(1,128)S(1)} all-to-all(f32[64,1,256]{2,1,0:T(1,128)S(1)} %broadcast_in_dim.9), channel_id=1, replica_groups=mesh['dp_0'=4,'dp_1'=8,'dp_2'=2,'mp'=8] {'dp_0','dp_1','dp_2'}, dimensions={0} | all-to-all | bytes 131072 | tf_op jit(solution)/shard_map/all_to_all | solution.py:17
  79.8 36.2 %all_to_all.47.second_ref = bf16[8,64,1136]{2,1,0:T(8,128)(2,1)S(1)} all-to-all(bf16[8,64,1136]{2,1,0:T(8,128)(2,1)S(1)} %factors.1), channel_id=1, replica_groups=mesh['dp_0'=4,'dp_1'=8,'dp_2'=2,'mp'=8] {'mp'}, dimensions={0} | all-to-all | bytes 2326528 | tf_op jit(solution)/shard_map/all_to_all | solution.py:17
  115.9 0.9 q_part.1
  117.0 17.0 %all_to_all.48 = f32[64,1,496]{2,1,0:T(1,128)S(1)} all-to-all(f32[64,1,496]{2,1,0:T(1,128)S(1)} %copy.14), channel_id=1, replica_groups=mesh['dp_0'=4,'dp_1'=8,'dp_2'=2,'mp'=8] {'dp_0','dp_1','dp_2'}, dimensions={0} | all-to-all | bytes 253952 | tf_op jit(solution)/shard_map/all_to_all | solution.py:17
  134.9 4.9 %all-to-all-start.4 = ((f32[64,1,496]{2,1,0:T(1,128)}), f32[64,1,496]{2,1,0:T(1,128)S(1)}, u32[]{:S(2)}, u32[]{:S(2)}) async-start(f32[64,1,496]{2,1,0:T(1,128)} %broadcast_in_dim.10), calls=%async_computation.4 | async-start | bytes 262144 | tf_op jit(solution)/shard_map/all_to_all | solution.py:17
  139.7 5.5 %inverse.1 = f32[64,64]{1,0:T(8,128)S(1)} custom-call(f32[64,64]{1,0:T(8,128)S(1)} %get-tuple-element.9.gram_ref), custom_call_target="tpu_custom_call" | custom-call | flops 1048576 | bytes 32768 | tf_op jit(solution)/shard_map/inverse/pallas_call | solution.py:35
  145.2 4.8 %all-to-all-done.4 = f32[64,1,496]{2,1,0:T(1,128)S(1)} async-done(((f32[64,1,496]{2,1,0:T(1,128)}), f32[64,1,496]{2,1,0:T(1,128)S(1)}, u32[]{:S(2)}, u32[]{:S(2)}) %all-to-all-start.4) | async-done | bytes 127008 | tf_op jit(solution)/shard_map/all_to_all | solution.py:17
  150.1 0.9 fusion.4
  151.0 0.8 broadcast_in_dim.11
  151.8 3.5 %all-to-all-start.5 = ((bf16[8,64,496]{2,1,0:T(8,128)(2,1)}), bf16[8,64,496]{2,1,0:T(8,128)(2,1)S(1)}, u32[]{:S(2)}, u32[]{:S(2)}) async-start(bf16[8,64,496]{2,1,0:T(8,128)(2,1)} %broadcast_in_dim.11), calls=%async_computation.5 | async-start | bytes 1048576 | tf_op jit(solution)/shard_map/all_to_all | solution.py:17
  155.5 0.8 broadcast_multiply_fusion
  156.5 1.6 copy-done.7
  158.1 1.6 copy-done.8
  159.6 1.3 merged.1.merged_ref
  160.9 1.9 %copy-done.2 = f32[256,3968]{1,0:T(8,128)} copy-done((f32[256,3968]{1,0:T(8,128)}, f32[256,3968]{1,0:T(8,128)S(1)}, u32[]{:S(2)}) %copy-start.2) | copy-done | bytes 4063256
  162.8 10.4 %all-to-all-done.5.q_ref = bf16[8,64,496]{2,1,0:T(8,128)(2,1)S(1)} async-done(((bf16[8,64,496]{2,1,0:T(8,128)(2,1)}), bf16[8,64,496]{2,1,0:T(8,128)(2,1)S(1)}, u32[]{:S(2)}, u32[]{:S(2)}) %all-to-all-start.5) | async-done | bytes 507936 | tf_op jit(solution)/shard_map/all_to_all | solution.py:17
  173.2 2.1 %copy-done.3 = f32[256,3968]{1,0:T(8,128)S(1)} copy-done((f32[256,3968]{1,0:T(8,128)S(1)}, f32[256,3968]{1,0:T(8,128)}, u32[]{:S(2)}) %copy-start.3) | copy-done | bytes 4063256
  175.4 2.0 %residue.1 = bf16[256,3968]{1,0:T(8,128)(2,1)} custom-call(bf16[8,64,496]{2,1,0:T(8,128)(2,1)S(1)} %all-to-all-done.5.q_ref, bf16[256,64]{1,0:T(8,128)(2,1)S(1)} %copy.16.p_ref, f32[256,3968]{1,0:T(8,128)S(1)} %copy-done.3), custom_call_target="tpu_custom_call" | custom-call | flops 130023424 | bytes 6635520 | tf_op jit(solution)/shard_map/residue/pallas_call | solution.py:35
  (32 shorter events, 2.6 us)
Async XLA Ops:
  7.2 149.3 %all-gather.4.cloned.1.call-start = ((), (), s32[]{:S(2)}) async-start(), calls=%async_computation.6 | async-start | bytes 2285568 | tf_op jit(solution)/shard_map/all_gather | solution.py:181
  7.2 1.0 copy-start.4
  8.2 0.9 copy-start.9
  9.2 23.8 %copy-start.6 = (bf16[512,256]{1,0:T(8,128)(2,1)S(1)}, bf16[512,256]{1,0:T(8,128)(2,1)}, u32[]{:S(2)}) copy-start(bf16[512,256]{1,0:T(8,128)(2,1)} %g_ref.3) | copy-start | bytes 786436
  32.9 1.6 copy-start
  34.5 44.6 %copy-start.1 = (bf16[256,3968]{1,0:T(8,128)(2,1)S(1)}, bf16[256,3968]{1,0:T(8,128)(2,1)}, u32[]{:S(2)}) copy-start(bf16[256,3968]{1,0:T(8,128)(2,1)} %e_ref.5) | copy-start | bytes 6094852
  35.9 120.6 %all-gather.6.cloned.1.call-start = ((), (), s32[]{:S(2)}) async-start(), calls=%async_computation.7 | async-start | bytes 2285568 | tf_op jit(solution)/shard_map/all_gather | solution.py:203
  79.8 36.2 %copy-start.5 = (bf16[512,496]{0,1:T(8,128)(2,1)S(1)}, bf16[512,496]{0,1:T(8,128)(2,1)}, u32[]{:S(2)}) copy-start(bf16[512,496]{0,1:T(8,128)(2,1)} %param.4) | copy-start | bytes 1523716
  134.9 15.2 %all-to-all-start.4 = ((f32[64,1,496]{2,1,0:T(1,128)}), f32[64,1,496]{2,1,0:T(1,128)S(1)}, u32[]{:S(2)}, u32[]{:S(2)}) async-start(f32[64,1,496]{2,1,0:T(1,128)} %broadcast_in_dim.10), calls=%async_computation.4 | async-start | bytes 262144 | tf_op jit(solution)/shard_map/all_to_all | solution.py:17
  151.8 21.4 %all-to-all-start.5 = ((bf16[8,64,496]{2,1,0:T(8,128)(2,1)}), bf16[8,64,496]{2,1,0:T(8,128)(2,1)S(1)}, u32[]{:S(2)}, u32[]{:S(2)}) async-start(bf16[8,64,496]{2,1,0:T(8,128)(2,1)} %broadcast_in_dim.11), calls=%async_computation.5 | async-start | bytes 1048576 | tf_op jit(solution)/shard_map/all_to_all | solution.py:17
  156.5 1.6 copy-start.7
  158.1 1.6 copy-start.8
  160.9 1.9 %copy-start.2 = (f32[256,3968]{1,0:T(8,128)}, f32[256,3968]{1,0:T(8,128)S(1)}, u32[]{:S(2)}) copy-start(f32[256,3968]{1,0:T(8,128)S(1)} %merged.1.merged_ref) | copy-start | bytes 12189700
  173.2 2.2 %copy-start.3 = (f32[256,3968]{1,0:T(8,128)S(1)}, f32[256,3968]{1,0:T(8,128)}, u32[]{:S(2)}) copy-start(f32[256,3968]{1,0:T(8,128)} %copy-done.2) | copy-start | bytes 12189700
Sparse Core Ops, SparseCore 0:
  36.0 48.0 all-gather.3
  117.0 33.6 all-gather.5

commit v3 on v2

--- a/solution.py
+++ b/solution.py
@@ -57,10 +57,9 @@
     out_ref[:, tokens:] = high
 
 
-def p_body(first_ref, g_ref, e_ref, x_ref, out_ref, x_half_ref):
+def p_body(first_ref, g_ref, e_ref, out_ref):
     tokens = g_ref.shape[0]
     shards = first_ref.shape[0]
-    x_half_ref[...] = x_ref[:, : x_half_ref.shape[1]]
     xq = first_ref[0, :, :tokens].astype(F32)
     for i in range(1, shards):
         xq = xq + first_ref[i, :, :tokens].astype(F32)
@@ -68,35 +67,38 @@
     out_ref[...] = nn(xq.astype(BF16), g_ref[...]) + nt(q_full, e_ref[...])
 
 
-def factors_body(p_ref, g_ref, e_ref, out_ref):
-    tokens = g_ref.shape[0]
-    shards, rank, width = out_ref.shape
-    cols = width - tokens - 2 * rank
+def column_tiles(width, tile=512):
+    return [(start, min(start + tile, width)) for start in range(0, width, tile)]
+
+
+def merged_body(p_ref, g_ref, e_ref, x_ref, out_ref, merged_ref):
+    shards, rank, size = out_ref.shape
+    cols = size - 2 * rank
     p = p_ref[...]
     p_b = p.astype(BF16)
     gram = nt(p, p, precision=HIGHEST)
     high = gram.astype(BF16)
     low = (gram - high.astype(F32)).astype(BF16)
-    gp = nt(p_b, g_ref[...]).astype(BF16)
-    ep = nn(p_b, e_ref[...]).astype(BF16)
     both = jnp.concatenate([high, low], axis=1)
+    g = g_ref[...]
+    parts = []
+    for lo, hi in column_tiles(e_ref.shape[1]):
+        merged = (nt(g, x_ref[lo:hi, :]) + e_ref[:, lo:hi].astype(F32)).astype(BF16)
+        merged_ref[:, lo:hi] = merged
+        parts.append(nn(p_b, merged).astype(BF16))
+    q_part = jnp.concatenate(parts, axis=1)
     for i in range(shards):
-        out_ref[i, :, :tokens] = gp
-        out_ref[i, :, tokens : tokens + 2 * rank] = both
-        out_ref[i, :, tokens + 2 * rank :] = ep[:, i * cols : (i + 1) * cols]
-
-
-def q_body(second_ref, x_ref, out_ref, gram_ref, x_half_ref):
-    tokens = x_ref.shape[1]
+        out_ref[i, :, : 2 * rank] = both
+        out_ref[i, :, 2 * rank :] = q_part[:, i * cols : (i + 1) * cols]
+
+
+def total_body(second_ref, out_ref, gram_ref):
     rank = out_ref.shape[0]
-    half = x_half_ref.shape[1]
-    x_half_ref[...] = x_ref[:, half:]
     total = second_ref[0].astype(F32)
     for i in range(1, second_ref.shape[0]):
         total = total + second_ref[i].astype(F32)
-    both = total[:, tokens : tokens + 2 * rank]
-    gram_ref[...] = both[:, :rank] + both[:, rank:]
-    out_ref[...] = nt(total[:, :tokens].astype(BF16), x_ref[...]) + total[:, tokens + 2 * rank :]
+    gram_ref[...] = total[:, :rank] + total[:, rank : 2 * rank]
+    out_ref[...] = total[:, 2 * rank :]
 
 
 def inverse_body(gram_ref, out_ref):
@@ -129,24 +131,13 @@
     out_ref[...] = jnp.concatenate(done, axis=0)
 
 
-def column_tiles(width, tile=512):
-    return [(start, min(start + tile, width)) for start in range(0, width, tile)]
-
-
-def merged_body(g_ref, e_ref, xa_ref, xb_ref, out_ref):
-    half = xa_ref.shape[1]
-    for lo, hi in column_tiles(e_ref.shape[1]):
-        made = nt(g_ref[:, :half], xa_ref[lo:hi, :]) + nt(g_ref[:, half:], xb_ref[lo:hi, :])
-        out_ref[:, lo:hi] = made + e_ref[:, lo:hi].astype(F32)
-
-
 def residue_body(q_ref, p_ref, merged_ref, out_ref):
     shards = q_ref.shape[0]
     q_full = jnp.concatenate([q_ref[i] for i in range(shards)], axis=1)
     p_rows = p_ref[...]
     for lo, hi in column_tiles(merged_ref.shape[1]):
         approx = nn(p_rows, q_full[:, lo:hi])
-        out_ref[:, lo:hi] = (merged_ref[:, lo:hi] - approx).astype(BF16)
+        out_ref[:, lo:hi] = (merged_ref[:, lo:hi].astype(F32) - approx).astype(BF16)
 
 
 def per_device(inputs, grad_out, error, q_prev):
@@ -155,9 +146,9 @@
     tokens, cols = inputs.shape
     rows = grad_out.shape[1]
     rank = q_prev.shape[1]
-    half = tokens // 2
     width = error.shape[1]
     x_t = inputs.T
+    x_full = lax.all_gather(x_t, "mp", axis=0, tiled=True)
 
     (packed,) = local_call(
         start_body,
@@ -168,39 +159,32 @@
         flops=4 * rank * tokens * cols,
     )
     first = lax.all_gather(packed, "mp")
-    p_part, x_a = local_call(
+    (p_part,) = local_call(
         p_body,
         "p_part",
-        [shaped((rank, rows), F32), shaped((cols, half), BF16)],
+        [shaped((rank, rows), F32)],
         first,
         grad_out,
         error,
-        x_t,
         flops=2 * rank * rows * (tokens + width),
     )
-    x_a = lax.all_gather(x_a, "mp", axis=0, tiled=True)
     p_row = jnp.sum(exchange(p_part, DP), axis=0) / replicas
     p_t = sent_to_all(p_row, DP)
 
-    (pieces,) = local_call(
-        factors_body,
-        "factors",
-        [shaped((shards, rank, tokens + 2 * rank + cols), BF16)],
+    pieces, merged = local_call(
+        merged_body,
+        "merged",
+        [shaped((shards, rank, 2 * rank + cols), BF16), shaped((rows, width), BF16)],
         p_t,
-        grad_out,
+        grad_out.T,
         error,
-        flops=2 * rank * rows * (tokens + width),
+        x_full,
+        flops=2 * rows * width * (tokens + rank),
     )
     second = exchange(pieces, "mp")
-    q_part, gram, x_b = local_call(
-        q_body,
-        "q_part",
-        [shaped((rank, cols), F32), shaped((rank, rank), F32), shaped((cols, half), BF16)],
-        second,
-        x_t,
-        flops=2 * rank * cols * tokens,
-    )
-    x_b = lax.all_gather(x_b, "mp", axis=0, tiled=True)
+    q_part, gram = local_call(
+        total_body, "total", [shaped((rank, cols), F32), shaped((rank, rank), F32)], second
+    )
     q_row = jnp.sum(exchange(q_part, DP), axis=0) / replicas
     mixed = sent_to_all(q_row, DP)
 
@@ -211,16 +195,6 @@
     q_own = nn(inverse, mixed, precision=HIGHEST)
 
     q_parts = sent_to_all(q_own.astype(BF16), "mp")
-    (merged,) = local_call(
-        merged_body,
-        "merged",
-        [shaped((rows, width), F32)],
-        grad_out.T,
-        error,
-        x_a,
-        x_b,
-        flops=2 * rows * width * tokens,
-    )
     (new_error,) = local_call(
         residue_body,
         "residue",

time: 185 us -> 176 us (0.951)
  blocking collectives: 120 us -> 95.1 us
  waiting for transfers between devices: 15.3 us -> 32.2 us
  local copies, waits for them, and re-layouts: 12.8 us -> 8.07 us
  starting transfers between devices: 8.45 us -> 12.9 us
    all_to_all x4 -> x3, blocking collectives: 96 us -> 70.5 us  [exchange(): return lax.all_to_all(pieces, axes, split_axis=0, concat_axis=0, tiled=True)]
    all_to_all x2 -> x3, waiting for transfers between devices: 15.2 us -> 31.5 us  [exchange(): return lax.all_to_all(pieces, axes, split_axis=0, concat_axis=0, tiled=True)]
    unnamed x22 -> x16, local copies, waits for them, and re-layouts: 10.8 us -> 5.52 us
    all_to_all x2 -> x3, starting transfers between devices: 8.37 us -> 12.8 us  [exchange(): return lax.all_to_all(pieces, axes, split_axis=0, concat_axis=0, tiled=True)]
    pallas_call x7 -> x6, Pallas kernels: 12.1 us -> 11.6 us  [local_call(): pl.pallas_call(body, name=name, out_shape=list(outs), in_specs=[spec] * l...]
  transfers between devices with their start and end apart: 4 -> 4, of which waited for: 2 -> 3; matrix products, arithmetic and copies ran while one was open for 2% -> 1% of each run, Pallas kernels for 5% -> 4%
where the time goes in v3:
time: 176 us
  blocking collectives  95.1 us (54%)
  waiting for transfers between devices  32.2 us (18%)
  between operations  14.1 us (8%)
  starting transfers between devices  12.9 us (7%)
  Pallas kernels  11.6 us (7%)
  local copies, waits for them, and re-layouts  8.07 us (5%)
    all_to_all x3, blocking collectives, exchange(): return lax.all_to_all(pieces, axes, split_axis=0, concat_axis=0, tiled=True)  70.5 us
    all_to_all x3, waiting for transfers between devices, exchange(): return lax.all_to_all(pieces, axes, split_axis=0, concat_axis=0, tiled=True)  31.5 us
    all_gather x1, blocking collectives, per_device(): first = lax.all_gather(packed, 'mp')  24.6 us
    all_to_all x3, starting transfers between devices, exchange(): return lax.all_to_all(pieces, axes, split_axis=0, concat_axis=0, tiled=True)  12.8 us
    pallas_call x6, Pallas kernels, local_call(): pl.pallas_call(body, name=name, out_shape=list(outs), in_specs=[spec] * l...  11.6 us
    unnamed x16, local copies, waits for them, and re-layouts  5.52 us
  transfers between devices with their start and end apart: 4, of which 3 were waited for; matrix products, arithmetic and copies ran while one was open for 1% of the time, Pallas kernels for 4%

profile of v3, /device:TPU:1, one launch (start us, length us, event | category | flops | bytes accessed | tf_op | source)
XLA Modules:
  0.0 176.0 jit_solution(8433444868849513937)
XLA Ops:
  7.2 0.7 all-gather.3.cloned.1.call-update
  7.9 1.0 copy-done.4
  8.9 0.9 copy-done.6
  10.1 24.6 %all-gather = bf16[512,1008]{1,0:T(8,128)(2,1)S(1)} all-gather(bf16[64,1008]{1,0:T(8,128)(2,1)S(1)} %start.1), channel_id=2, replica_groups=mesh['dp_0'=4,'dp_1'=8,'dp_2'=2,'mp'=8] {'mp'}, dimensions={0}, use_global_device_ids=true | all-gather | bytes 1161216 | tf_op jit(solution)/shard_map/all_gather | solution.py:161
  34.8 0.8 p_part.1
  35.7 31.2 %all_to_all.45 = f32[64,1,256]{2,1,0:T(1,128)S(1)} all-to-all(f32[64,1,256]{2,1,0:T(1,128)S(1)} %copy.13), channel_id=1, replica_groups=mesh['dp_0'=4,'dp_1'=8,'dp_2'=2,'mp'=8] {'dp_0','dp_1','dp_2'}, dimensions={0} | all-to-all | bytes 131072 | tf_op jit(solution)/shard_map/all_to_all | solution.py:17
  66.9 0.7 broadcast_in_dim.9
  67.6 4.4 %all-to-all-start.1 = ((f32[64,1,256]{2,1,0:T(1,128)}), f32[64,1,256]{2,1,0:T(1,128)S(1)}, u32[]{:S(2)}, u32[]{:S(2)}) async-start(f32[64,1,256]{2,1,0:T(1,128)} %broadcast_in_dim.9), calls=%async_computation.1 | async-start | bytes 131072 | tf_op jit(solution)/shard_map/all_to_all | solution.py:17
  72.2 9.7 %all-to-all-done.1 = f32[64,1,256]{2,1,0:T(1,128)S(1)} async-done(((f32[64,1,256]{2,1,0:T(1,128)}), f32[64,1,256]{2,1,0:T(1,128)S(1)}, u32[]{:S(2)}, u32[]{:S(2)}) %all-to-all-start.1) | async-done | bytes 65568 | tf_op jit(solution)/shard_map/all_to_all | solution.py:17
  82.0 2.1 %copy-done.1 = bf16[3968,512]{1,0:T(8,128)(2,1)S(1)} copy-done((bf16[3968,512]{1,0:T(8,128)(2,1)S(1)}, bf16[3968,512]{1,0:T(8,128)(2,1)}, u32[]{:S(2)}) %copy-start.1) | copy-done | bytes 4063256
  84.1 2.9 %merged.1 = (bf16[8,64,624]{2,1,0:T(8,128)(2,1)S(1)}, bf16[256,3968]{1,0:T(8,128)(2,1)S(1)}) custom-call(f32[64,256]{1,0:T(8,128)S(1)} %bitcast.24, bf16[256,512]{1,0:T(8,128)(2,1)S(1)} %bitcast.23, bf16[256,3968]{1,0:T(8,128)(2,1)S(1)} %copy-done, bf16[3968,512]{1,0:T(8,128)(2,1)S(1)} %copy-done.1), custom_call_target="tpu_custom_call" | custom-call | flops 1170210816 | bytes 9093120 | tf_op jit(solution)/shard_map/merged/pallas_call | solution.py:35
  87.0 1.3 copy-done.2
  88.3 23.6 %all_to_all.46.second_ref = bf16[8,64,624]{2,1,0:T(8,128)(2,1)S(1)} all-to-all(bf16[8,64,624]{2,1,0:T(8,128)(2,1)S(1)} %get-tuple-element.7), channel_id=1, replica_groups=mesh['dp_0'=4,'dp_1'=8,'dp_2'=2,'mp'=8] {'mp'}, dimensions={0} | all-to-all | bytes 1277952 | tf_op jit(solution)/shard_map/all_to_all | solution.py:17
  112.2 15.7 %all_to_all.47 = f32[64,1,496]{2,1,0:T(1,128)S(1)} all-to-all(f32[64,1,496]{2,1,0:T(1,128)S(1)} %copy.15), channel_id=1, replica_groups=mesh['dp_0'=4,'dp_1'=8,'dp_2'=2,'mp'=8] {'dp_0','dp_1','dp_2'}, dimensions={0} | all-to-all | bytes 253952 | tf_op jit(solution)/shard_map/all_to_all | solution.py:17
  128.0 0.7 broadcast_in_dim.10
  128.8 4.9 %all-to-all-start.4 = ((f32[64,1,496]{2,1,0:T(1,128)}), f32[64,1,496]{2,1,0:T(1,128)S(1)}, u32[]{:S(2)}, u32[]{:S(2)}) async-start(f32[64,1,496]{2,1,0:T(1,128)} %broadcast_in_dim.10), calls=%async_computation.4 | async-start | bytes 262144 | tf_op jit(solution)/shard_map/all_to_all | solution.py:17
  133.6 5.5 %inverse.1 = f32[64,64]{1,0:T(8,128)S(1)} custom-call(f32[64,64]{1,0:T(8,128)S(1)} %get-tuple-element.8.gram_ref), custom_call_target="tpu_custom_call" | custom-call | flops 1048576 | bytes 32768 | tf_op jit(solution)/shard_map/inverse/pallas_call | solution.py:35
  139.1 4.8 %all-to-all-done.4 = f32[64,1,496]{2,1,0:T(1,128)S(1)} async-done(((f32[64,1,496]{2,1,0:T(1,128)}), f32[64,1,496]{2,1,0:T(1,128)S(1)}, u32[]{:S(2)}, u32[]{:S(2)}) %all-to-all-start.4) | async-done | bytes 127008 | tf_op jit(solution)/shard_map/all_to_all | solution.py:17
  144.0 0.9 fusion.4
  144.9 0.8 broadcast_in_dim.11
  145.7 3.5 %all-to-all-start.5 = ((bf16[8,64,496]{2,1,0:T(8,128)(2,1)}), bf16[8,64,496]{2,1,0:T(8,128)(2,1)S(1)}, u32[]{:S(2)}, u32[]{:S(2)}) async-start(bf16[8,64,496]{2,1,0:T(8,128)(2,1)} %broadcast_in_dim.11), calls=%async_computation.5 | async-start | bytes 1048576 | tf_op jit(solution)/shard_map/all_to_all | solution.py:17
  149.2 0.8 broadcast_multiply_fusion
  150.2 16.9 %all-to-all-done.5.q_ref = bf16[8,64,496]{2,1,0:T(8,128)(2,1)S(1)} async-done(((bf16[8,64,496]{2,1,0:T(8,128)(2,1)}), bf16[8,64,496]{2,1,0:T(8,128)(2,1)S(1)}, u32[]{:S(2)}, u32[]{:S(2)}) %all-to-all-start.5) | async-done | bytes 507936 | tf_op jit(solution)/shard_map/all_to_all | solution.py:17
  167.1 2.0 %residue.1 = bf16[256,3968]{1,0:T(8,128)(2,1)} custom-call(bf16[8,64,496]{2,1,0:T(8,128)(2,1)S(1)} %all-to-all-done.5.q_ref, bf16[256,64]{1,0:T(8,128)(2,1)S(1)} %copy.16.p_ref, bf16[256,3968]{1,0:T(8,128)(2,1)S(1)} %copy-done.3), custom_call_target="tpu_custom_call" | custom-call | flops 130023424 | bytes 4603904 | tf_op jit(solution)/shard_map/residue/pallas_call | solution.py:35
  (23 shorter events, 1.2 us)
Async XLA Ops:
  7.2 27.6 %copy-start = (bf16[256,3968]{1,0:T(8,128)(2,1)S(1)}, bf16[256,3968]{1,0:T(8,128)(2,1)}, u32[]{:S(2)}) copy-start(bf16[256,3968]{1,0:T(8,128)(2,1)} %e_ref.3) | copy-start | bytes 6094852
  7.2 74.8 %all-gather.3.cloned.1.call-start = ((), (), s32[]{:S(2)}) async-start(), calls=%async_computation.6 | async-start | bytes 4571136 | tf_op jit(solution)/shard_map/all_gather | solution.py:151
  7.9 1.0 copy-start.4
  8.9 0.9 copy-start.6
  9.9 24.9 %copy-start.5 = (bf16[512,256]{1,0:T(8,128)(2,1)S(1)}, bf16[512,256]{1,0:T(8,128)(2,1)}, u32[]{:S(2)}) copy-start(bf16[512,256]{1,0:T(8,128)(2,1)} %g_ref.1) | copy-start | bytes 786436
  67.6 14.3 %all-to-all-start.1 = ((f32[64,1,256]{2,1,0:T(1,128)}), f32[64,1,256]{2,1,0:T(1,128)S(1)}, u32[]{:S(2)}, u32[]{:S(2)}) async-start(f32[64,1,256]{2,1,0:T(1,128)} %broadcast_in_dim.9), calls=%async_computation.1 | async-start | bytes 131072 | tf_op jit(solution)/shard_map/all_to_all | solution.py:17
  81.9 2.2 %copy-start.1 = (bf16[3968,512]{1,0:T(8,128)(2,1)S(1)}, bf16[3968,512]{1,0:T(8,128)(2,1)}, u32[]{:S(2)}) copy-start(bf16[3968,512]{1,0:T(8,128)(2,1)} %all-gather.3.cloned.1.call-done.x_ref) | copy-start | bytes 12189700
  87.0 1.3 copy-start.2
  111.9 55.2 %copy-start.3 = (bf16[256,3968]{1,0:T(8,128)(2,1)S(1)}, bf16[256,3968]{1,0:T(8,128)(2,1)}, u32[]{:S(2)}) copy-start(bf16[256,3968]{1,0:T(8,128)(2,1)} %copy-done.2) | copy-start | bytes 6094852
  128.8 15.2 %all-to-all-start.4 = ((f32[64,1,496]{2,1,0:T(1,128)}), f32[64,1,496]{2,1,0:T(1,128)S(1)}, u32[]{:S(2)}, u32[]{:S(2)}) async-start(f32[64,1,496]{2,1,0:T(1,128)} %broadcast_in_dim.10), calls=%async_computation.4 | async-start | bytes 262144 | tf_op jit(solution)/shard_map/all_to_all | solution.py:17
  145.7 21.4 %all-to-all-start.5 = ((bf16[8,64,496]{2,1,0:T(8,128)(2,1)}), bf16[8,64,496]{2,1,0:T(8,128)(2,1)S(1)}, u32[]{:S(2)}, u32[]{:S(2)}) async-start(bf16[8,64,496]{2,1,0:T(8,128)(2,1)} %broadcast_in_dim.11), calls=%async_computation.5 | async-start | bytes 1048576 | tf_op jit(solution)/shard_map/all_to_all | solution.py:17
Sparse Core Ops, SparseCore 0:
  10.1 63.7 all-gather.2

commit v4 on v3

--- a/solution.py
+++ b/solution.py
@@ -7,10 +7,14 @@
 from jax.sharding import PartitionSpec as P
 
 DP = ("dp_0", "dp_1", "dp_2")
+CHIPS = ("dp_0", "dp_1")
+CORE = "dp_2"
 DP_MP = ("dp_0", "dp_1", "dp_2", "mp")
 BF16 = jnp.bfloat16
 F32 = jnp.float32
 HIGHEST = lax.Precision.HIGHEST
+GRANT = 16 * 1024 * 1024
+WIDE_GRANT = 60 * 1024 * 1024
 
 
 def exchange(pieces, axes):
@@ -29,16 +33,15 @@
     return lax.dot_general(a, b, (((1,), (0,)), ((), ())), preferred_element_type=F32, **kw)
 
 
-def local_call(body, name, outs, *args, flops=0):
+def local_call(body, outs, *args, flops=0):
     spec = pl.BlockSpec(memory_space=pltpu.VMEM)
     moved = sum(a.size * a.dtype.itemsize for a in (*args, *outs))
     return pl.pallas_call(
         body,
-        name=name,
         out_shape=list(outs),
         in_specs=[spec] * len(args),
         out_specs=[spec] * len(outs),
-        compiler_params=pltpu.CompilerParams(vmem_limit_bytes=16 * 1024 * 1024),
+        compiler_params=pltpu.CompilerParams(vmem_limit_bytes=GRANT),
         cost_estimate=pl.CostEstimate(flops=flops, bytes_accessed=moved, transcendentals=0),
     )(*args)
 
@@ -71,34 +74,86 @@
     return [(start, min(start + tile, width)) for start in range(0, width, tile)]
 
 
-def merged_body(p_ref, g_ref, e_ref, x_ref, out_ref, merged_ref):
-    shards, rank, size = out_ref.shape
-    cols = size - 2 * rank
+def merged_body(g_ref, e_hbm, x_hbm, out_ref, e_ref, x_ref, sems):
+    copies = []
+    for i, (lo, hi) in enumerate(column_tiles(out_ref.shape[1])):
+        pair = (
+            pltpu.make_async_copy(x_hbm.at[lo:hi, :], x_ref.at[lo:hi, :], sems.at[0, i]),
+            pltpu.make_async_copy(e_hbm.at[:, lo:hi], e_ref.at[:, lo:hi], sems.at[1, i]),
+        )
+        for copy in pair:
+            copy.start()
+        copies.append(pair)
+    g = g_ref[...]
+    for (lo, hi), pair in zip(column_tiles(out_ref.shape[1]), copies):
+        for copy in pair:
+            copy.wait()
+        made = nt(g, x_ref[lo:hi, :]) + e_ref[:, lo:hi].astype(F32)
+        out_ref[:, lo:hi] = made.astype(BF16)
+
+
+def merge(g_t, error, x_full):
+    rows, width = error.shape
+    return pl.pallas_call(
+        merged_body,
+        name="merged",
+        out_shape=shaped((rows, width), BF16),
+        in_specs=[
+            pl.BlockSpec(memory_space=pltpu.VMEM),
+            pl.BlockSpec(memory_space=pltpu.HBM),
+            pl.BlockSpec(memory_space=pltpu.HBM),
+        ],
+        out_specs=pl.BlockSpec(memory_space=pltpu.VMEM),
+        scratch_shapes=[
+            pltpu.VMEM(error.shape, error.dtype),
+            pltpu.VMEM(x_full.shape, x_full.dtype),
+            pltpu.SemaphoreType.DMA((2, len(column_tiles(width)))),
+        ],
+        compiler_params=pltpu.CompilerParams(vmem_limit_bytes=WIDE_GRANT),
+        cost_estimate=pl.CostEstimate(
+            flops=2 * rows * width * g_t.shape[1],
+            bytes_accessed=4 * rows * width + 2 * x_full.size,
+            transcendentals=0,
+        ),
+    )(g_t, error, x_full)
+
+
+def product_body(p_ref, merged_ref, out_ref, gram_ref):
+    rank = p_ref.shape[0]
     p = p_ref[...]
-    p_b = p.astype(BF16)
     gram = nt(p, p, precision=HIGHEST)
     high = gram.astype(BF16)
-    low = (gram - high.astype(F32)).astype(BF16)
-    both = jnp.concatenate([high, low], axis=1)
-    g = g_ref[...]
-    parts = []
-    for lo, hi in column_tiles(e_ref.shape[1]):
-        merged = (nt(g, x_ref[lo:hi, :]) + e_ref[:, lo:hi].astype(F32)).astype(BF16)
-        merged_ref[:, lo:hi] = merged
-        parts.append(nn(p_b, merged).astype(BF16))
-    q_part = jnp.concatenate(parts, axis=1)
+    gram_ref[:, :rank] = high
+    gram_ref[:, rank:] = (gram - high.astype(F32)).astype(BF16)
+    row = lax.broadcasted_iota(jnp.int32, (rank, rank), 0)
+    col = lax.broadcasted_iota(jnp.int32, (rank, rank), 1)
+    near = rank // 2
+    evens_first = jnp.where(row < near, 2 * row, 2 * (row - near) + 1)
+    p_b = nn((col == evens_first).astype(BF16), p.astype(BF16)).astype(BF16)
+    for lo, hi in column_tiles(merged_ref.shape[1]):
+        out_ref[:, lo:hi] = nn(p_b, merged_ref[:, lo:hi]).astype(BF16)
+
+
+def pack_body(pair_ref, gram_ref, out_ref):
+    _, width = gram_ref.shape
+    shards, near, size = out_ref.shape
+    both = jnp.concatenate([gram_ref[:near, :], gram_ref[near:, :]], axis=1)
+    summed = (pair_ref[:near, :].astype(F32) + pair_ref[near:, :].astype(F32)).astype(BF16)
+    cols = size - 2 * width
     for i in range(shards):
-        out_ref[i, :, : 2 * rank] = both
-        out_ref[i, :, 2 * rank :] = q_part[:, i * cols : (i + 1) * cols]
+        out_ref[i, :, : 2 * width] = both
+        out_ref[i, :, 2 * width :] = summed[:, i * cols : (i + 1) * cols]
 
 
 def total_body(second_ref, out_ref, gram_ref):
-    rank = out_ref.shape[0]
+    near = out_ref.shape[0]
+    rank = gram_ref.shape[0]
     total = second_ref[0].astype(F32)
     for i in range(1, second_ref.shape[0]):
         total = total + second_ref[i].astype(F32)
-    gram_ref[...] = total[:, :rank] + total[:, rank : 2 * rank]
-    out_ref[...] = total[:, 2 * rank :]
+    gram_ref[:near, :] = total[:, :rank] + total[:, rank : 2 * rank]
+    gram_ref[near:, :] = total[:, 2 * rank : 3 * rank] + total[:, 3 * rank : 4 * rank]
+    out_ref[...] = total[:, 4 * rank :]
 
 
 def inverse_body(gram_ref, out_ref):
@@ -131,16 +186,45 @@
     out_ref[...] = jnp.concatenate(done, axis=0)
 
 
-def residue_body(q_ref, p_ref, merged_ref, out_ref):
+def residue_body(q_ref, p_ref, merged_ref, out_hbm, out_ref, sems):
     shards = q_ref.shape[0]
     q_full = jnp.concatenate([q_ref[i] for i in range(shards)], axis=1)
     p_rows = p_ref[...]
-    for lo, hi in column_tiles(merged_ref.shape[1]):
+    copies = []
+    for i, (lo, hi) in enumerate(column_tiles(merged_ref.shape[1])):
         approx = nn(p_rows, q_full[:, lo:hi])
         out_ref[:, lo:hi] = (merged_ref[:, lo:hi].astype(F32) - approx).astype(BF16)
-
-
-def per_device(inputs, grad_out, error, q_prev):
+        copies.append(
+            pltpu.make_async_copy(out_ref.at[:, lo:hi], out_hbm.at[:, lo:hi], sems.at[i])
+        )
+        copies[-1].start()
+    for copy in copies:
+        copy.wait()
+
+
+def residue(q_parts, p_rows, merged):
+    rows, width = merged.shape
+    spec = pl.BlockSpec(memory_space=pltpu.VMEM)
+    return pl.pallas_call(
+        residue_body,
+        name="residue",
+        out_shape=shaped((rows, width), BF16),
+        in_specs=[spec] * 3,
+        out_specs=pl.BlockSpec(memory_space=pltpu.HBM),
+        scratch_shapes=[
+            pltpu.VMEM((rows, width), BF16),
+            pltpu.SemaphoreType.DMA((len(column_tiles(width)),)),
+        ],
+        compiler_params=pltpu.CompilerParams(vmem_limit_bytes=GRANT),
+        cost_estimate=pl.CostEstimate(
+            flops=2 * rows * width * p_rows.shape[1],
+            bytes_accessed=4 * rows * width,
+            transcendentals=0,
+        ),
+    )(q_parts, p_rows, merged)
+
+
+def layer(inputs, grad_out, error, q_prev):
     replicas = lax.axis_size(DP)
     shards = lax.axis_size("mp")
     tokens, cols = inputs.shape
@@ -152,7 +236,6 @@
 
     (packed,) = local_call(
         start_body,
-        "start",
         [shaped((rank, tokens + cols), BF16)],
         x_t,
         q_prev.T,
@@ -161,7 +244,6 @@
     first = lax.all_gather(packed, "mp")
     (p_part,) = local_call(
         p_body,
-        "p_part",
         [shaped((rank, rows), F32)],
         first,
         grad_out,
@@ -171,39 +253,33 @@
     p_row = jnp.sum(exchange(p_part, DP), axis=0) / replicas
     p_t = sent_to_all(p_row, DP)
 
-    pieces, merged = local_call(
-        merged_body,
-        "merged",
-        [shaped((shards, rank, 2 * rank + cols), BF16), shaped((rows, width), BF16)],
+    merged = merge(grad_out.T, error, x_full)
+    product, gram_part = local_call(
+        product_body,
+        [shaped((rank, width), BF16), shaped((rank, 2 * rank), BF16)],
         p_t,
-        grad_out.T,
-        error,
-        x_full,
-        flops=2 * rows * width * (tokens + rank),
-    )
-    second = exchange(pieces, "mp")
+        merged,
+        flops=2 * rows * width * rank,
+    )
+    near = rank // lax.axis_size(CORE)
+    (pieces,) = local_call(
+        pack_body,
+        [shaped((shards, near, 4 * rank + cols), BF16)],
+        exchange(product, CORE),
+        gram_part,
+    )
     q_part, gram = local_call(
-        total_body, "total", [shaped((rank, cols), F32), shaped((rank, rank), F32)], second
-    )
-    q_row = jnp.sum(exchange(q_part, DP), axis=0) / replicas
+        total_body, [shaped((near, cols), F32), shaped((rank, rank), F32)], exchange(pieces, "mp")
+    )
+    q_row = jnp.sum(exchange(q_part, CHIPS), axis=0) / replicas
     mixed = sent_to_all(q_row, DP)
 
-    (inverse,) = local_call(
-        inverse_body, "inverse", [shaped((rank, rank), F32)], gram, flops=4 * rank**3
-    )
+    (inverse,) = local_call(inverse_body, [shaped((rank, rank), F32)], gram, flops=4 * rank**3)
     p_hat = nn(inverse, p_t, precision=HIGHEST)
     q_own = nn(inverse, mixed, precision=HIGHEST)
 
     q_parts = sent_to_all(q_own.astype(BF16), "mp")
-    (new_error,) = local_call(
-        residue_body,
-        "residue",
-        [shaped((rows, width), BF16)],
-        q_parts,
-        p_hat.astype(BF16).T,
-        merged,
-        flops=2 * rows * width * rank,
-    )
+    new_error = residue(q_parts, p_hat.astype(BF16).T, merged)
     scale = jnp.sqrt(F32(rows * shards))
     return (new_error, (p_hat * scale).T, q_own.T)
 
@@ -212,6 +288,4 @@
     finer = Mesh(mesh.devices.reshape(4, 8, 2, mesh.shape["mp"]), ("dp_0", "dp_1", "dp_2", "mp"))
     in_specs = (P(DP, "mp"), P(DP, "mp"), P(DP_MP, None), P("mp", None))
     out_specs = (P(DP_MP, None), P("mp", None), P("mp", None))
-    return jax.shard_map(
-        per_device, mesh=finer, in_specs=in_specs, out_specs=out_specs, check_vma=False
-    )
+    return jax.shard_map(layer, mesh=finer, in_specs=in_specs, out_specs=out_specs, check_vma=False)

time: 176 us -> 176 us (level)
  blocking collectives: 95.1 us -> 90.1 us
  Pallas kernels: 11.6 us -> 15.2 us
  starting transfers between devices: 12.9 us -> 15.2 us
    all_to_all x3 -> x4, blocking collectives: 70.5 us -> 65.4 us  [exchange(): return lax.all_to_all(pieces, axes, split_axis=0, concat_axis=0, tiled=True)]
    pallas_call x6 -> x8, Pallas kernels: 11.6 us -> 15.2 us  [the longest x6 7.35 us: local_call(): pl.pallas_call(body, out_shape=list(outs), in_specs=[spec] * len(args), o...]
    all_to_all x3, starting transfers between devices: 12.8 us -> 15.1 us  [exchange(): return lax.all_to_all(pieces, axes, split_axis=0, concat_axis=0, tiled=True)]
    unnamed x16 -> x14, local copies, waits for them, and re-layouts: 5.52 us -> 4.35 us
where the time goes in v4:
time: 176 us; the launch traced here: 175 us
  blocking collectives  90.1 us (51%)
  waiting for transfers between devices  31.6 us (18%)
  starting transfers between devices  15.2 us (9%)
  Pallas kernels  15.2 us (9%)
  between operations  14.2 us (8%)
  local copies, waits for them, and re-layouts  6.84 us (4%)
    all_to_all x4, blocking collectives, exchange(): return lax.all_to_all(pieces, axes, split_axis=0, concat_axis=0, tiled=True)  65.4 us
    all_to_all x3, waiting for transfers between devices, exchange(): return lax.all_to_all(pieces, axes, split_axis=0, concat_axis=0, tiled=True)  30.9 us
    all_gather x1, blocking collectives, layer(): first = lax.all_gather(packed, 'mp')  24.7 us
    all_to_all x3, starting transfers between devices, exchange(): return lax.all_to_all(pieces, axes, split_axis=0, concat_axis=0, tiled=True)  15.1 us
    pallas_call x6, Pallas kernels, local_call(): pl.pallas_call(body, out_shape=list(outs), in_specs=[spec] * len(args), o...  7.35 us
    pallas_call x1, Pallas kernels, merge(): pl.pallas_call(merged_body, name='merged', out_shape=shaped((rows, width)...  6.18 us
    unnamed x14, local copies, waits for them, and re-layouts  4.35 us
  transfers between devices with their start and end apart: 4, of which 3 were waited for; matrix products, arithmetic and copies ran while one was open for 1% of the time, Pallas kernels for 4%

profile of v4, /device:TPU:1, one launch (start us, length us, event | category | flops | bytes accessed | tf_op | source)
XLA Modules:
  0.0 175.0 jit_solution(13236443981304918231)
XLA Ops:
  7.2 0.7 all-gather.3.cloned.1.call-update
  7.9 1.0 copy-done.3
  8.9 0.9 copy-done.5
  10.1 24.7 %all-gather = bf16[512,1008]{1,0:T(8,128)(2,1)S(1)} all-gather(bf16[64,1008]{1,0:T(8,128)(2,1)S(1)} %shard_map.67), channel_id=2, replica_groups=mesh['dp_0'=4,'dp_1'=8,'dp_2'=2,'mp'=8] {'mp'}, dimensions={0}, use_global_device_ids=true | all-gather | bytes 1161216 | tf_op jit(solution)/shard_map/all_gather | solution.py:244
  34.8 0.8 shard_map.68
  35.7 31.1 %all_to_all.56 = f32[64,1,256]{2,1,0:T(1,128)S(1)} all-to-all(f32[64,1,256]{2,1,0:T(1,128)S(1)} %copy.13), channel_id=1, replica_groups=mesh['dp_0'=4,'dp_1'=8,'dp_2'=2,'mp'=8] {'dp_0','dp_1','dp_2'}, dimensions={0} | all-to-all | bytes 131072 | tf_op jit(solution)/shard_map/all_to_all | solution.py:21
  67.6 4.4 %all-to-all-start.1 = ((f32[64,1,256]{2,1,0:T(1,128)}), f32[64,1,256]{2,1,0:T(1,128)S(1)}, u32[]{:S(2)}, u32[]{:S(2)}) async-start(f32[64,1,256]{2,1,0:T(1,128)} %broadcast_in_dim.9), calls=%async_computation.1 | async-start | bytes 131072 | tf_op jit(solution)/shard_map/all_to_all | solution.py:21
  72.0 0.8 copy.14
  72.9 9.1 %all-to-all-done.1 = f32[64,1,256]{2,1,0:T(1,128)S(1)} async-done(((f32[64,1,256]{2,1,0:T(1,128)}), f32[64,1,256]{2,1,0:T(1,128)S(1)}, u32[]{:S(2)}, u32[]{:S(2)}) %all-to-all-start.1) | async-done | bytes 65568 | tf_op jit(solution)/shard_map/all_to_all | solution.py:21
  81.9 6.2 %merged.1.merged_ref = bf16[256,3968]{1,0:T(8,128)(2,1)} custom-call(bf16[256,512]{1,0:T(8,128)(2,1)} %bitcast.31, bf16[256,3968]{1,0:T(8,128)(2,1)} %e_hbm.1, bf16[3968,512]{1,0:T(8,128)(2,1)} %all-gather.3.cloned.1.call-done.x_hbm), custom_call_target="tpu_custom_call" | custom-call | flops 1040187392 | bytes 8126464 | tf_op jit(solution)/shard_map/merged/pallas_call | solution.py:97
  88.1 1.6 copy-done
  90.2 4.2 %all_to_all.57 = bf16[2,32,3968]{2,1,0:T(8,128)(2,1)S(1)} all-to-all(bf16[2,32,3968]{2,1,0:T(8,128)(2,1)S(1)} %bitcast.26), channel_id=1, replica_groups=mesh['dp_0'=4,'dp_1'=8,'dp_2'=2,'mp'=8] {'dp_2'}, dimensions={0} | all-to-all | bytes 1015808 | tf_op jit(solution)/shard_map/all_to_all | solution.py:21
  94.6 18.3 %all_to_all.58.second_ref = bf16[8,32,752]{2,1,0:T(8,128)(2,1)S(1)} all-to-all(bf16[8,32,752]{2,1,0:T(8,128)(2,1)S(1)} %shard_map.70), channel_id=1, replica_groups=mesh['dp_0'=4,'dp_1'=8,'dp_2'=2,'mp'=8] {'mp'}, dimensions={0} | all-to-all | bytes 770048 | tf_op jit(solution)/shard_map/all_to_all | solution.py:21
  113.0 11.9 %all_to_all.59 = f32[32,1,496]{2,1,0:T(1,128)S(1)} all-to-all(f32[32,1,496]{2,1,0:T(1,128)S(1)} %copy.15), channel_id=1, replica_groups=mesh['dp_0'=4,'dp_1'=8,'dp_2'=2,'mp'=8] {'dp_0','dp_1'}, dimensions={0} | all-to-all | bytes 126976 | tf_op jit(solution)/shard_map/all_to_all | solution.py:21
  124.9 0.7 broadcast_in_dim.10
  125.7 7.2 %all-to-all-start.5 = ((f32[64,1,496]{2,1,0:T(1,128)}), f32[64,1,496]{2,1,0:T(1,128)S(1)}, u32[]{:S(2)}, u32[]{:S(2)}) async-start(f32[64,1,496]{2,1,0:T(1,128)} %broadcast_in_dim.10), calls=%async_computation.5 | async-start | bytes 262144 | tf_op jit(solution)/shard_map/all_to_all | solution.py:21
  132.9 5.5 %shard_map.72 = f32[64,64]{1,0:T(8,128)S(1)} custom-call(f32[64,64]{1,0:T(8,128)S(1)} %get-tuple-element.9.gram_ref), custom_call_target="tpu_custom_call" | custom-call | flops 1048576 | bytes 32768 | tf_op jit(solution)/shard_map/pallas_call | solution.py:39
  138.4 5.0 %all-to-all-done.5 = f32[64,1,496]{2,1,0:T(1,128)S(1)} async-done(((f32[64,1,496]{2,1,0:T(1,128)}), f32[64,1,496]{2,1,0:T(1,128)S(1)}, u32[]{:S(2)}, u32[]{:S(2)}) %all-to-all-start.5) | async-done | bytes 127008 | tf_op jit(solution)/shard_map/all_to_all | solution.py:21
  143.3 0.9 fusion.4
  144.2 0.8 broadcast_in_dim.11
  145.1 3.5 %all-to-all-start.6 = ((bf16[8,64,496]{2,1,0:T(8,128)(2,1)}), bf16[8,64,496]{2,1,0:T(8,128)(2,1)S(1)}, u32[]{:S(2)}, u32[]{:S(2)}) async-start(bf16[8,64,496]{2,1,0:T(8,128)(2,1)} %broadcast_in_dim.11), calls=%async_computation.6 | async-start | bytes 1048576 | tf_op jit(solution)/shard_map/all_to_all | solution.py:21
  148.6 0.8 broadcast_multiply_fusion
  149.5 16.9 %all-to-all-done.6.q_ref = bf16[8,64,496]{2,1,0:T(8,128)(2,1)S(1)} async-done(((bf16[8,64,496]{2,1,0:T(8,128)(2,1)}), bf16[8,64,496]{2,1,0:T(8,128)(2,1)S(1)}, u32[]{:S(2)}, u32[]{:S(2)}) %all-to-all-start.6) | async-done | bytes 507936 | tf_op jit(solution)/shard_map/all_to_all | solution.py:21
  166.5 1.6 residue.1
  (24 shorter events, 2.2 us)
Async XLA Ops:
  7.2 27.7 %copy-start.2 = (bf16[256,3968]{1,0:T(8,128)(2,1)S(1)}, bf16[256,3968]{1,0:T(8,128)(2,1)}, u32[]{:S(2)}) copy-start(bf16[256,3968]{1,0:T(8,128)(2,1)} %e_hbm.1) | copy-start | bytes 6094852
  7.2 74.8 %all-gather.3.cloned.1.call-start = ((), (), s32[]{:S(2)}) async-start(), calls=%async_computation.7 | async-start | bytes 4571136 | tf_op jit(solution)/shard_map/all_gather | solution.py:235
  7.9 1.0 copy-start.3
  8.9 0.9 copy-start.5
  9.9 25.0 %copy-start.4 = (bf16[512,256]{1,0:T(8,128)(2,1)S(1)}, bf16[512,256]{1,0:T(8,128)(2,1)}, u32[]{:S(2)}) copy-start(bf16[512,256]{1,0:T(8,128)(2,1)} %g_ref.1) | copy-start | bytes 786436
  67.6 14.3 %all-to-all-start.1 = ((f32[64,1,256]{2,1,0:T(1,128)}), f32[64,1,256]{2,1,0:T(1,128)S(1)}, u32[]{:S(2)}, u32[]{:S(2)}) async-start(f32[64,1,256]{2,1,0:T(1,128)} %broadcast_in_dim.9), calls=%async_computation.1 | async-start | bytes 131072 | tf_op jit(solution)/shard_map/all_to_all | solution.py:21
  88.1 1.6 copy-start
  94.6 71.9 %copy-start.1 = (bf16[256,3968]{1,0:T(8,128)(2,1)S(1)}, bf16[256,3968]{1,0:T(8,128)(2,1)}, u32[]{:S(2)}) copy-start(bf16[256,3968]{1,0:T(8,128)(2,1)} %merged.1.merged_ref) | copy-start | bytes 6094852
  125.7 17.7 %all-to-all-start.5 = ((f32[64,1,496]{2,1,0:T(1,128)}), f32[64,1,496]{2,1,0:T(1,128)S(1)}, u32[]{:S(2)}, u32[]{:S(2)}) async-start(f32[64,1,496]{2,1,0:T(1,128)} %broadcast_in_dim.10), calls=%async_computation.5 | async-start | bytes 262144 | tf_op jit(solution)/shard_map/all_to_all | solution.py:21
  145.1 21.4 %all-to-all-start.6 = ((bf16[8,64,496]{2,1,0:T(8,128)(2,1)}), bf16[8,64,496]{2,1,0:T(8,128)(2,1)S(1)}, u32[]{:S(2)}, u32[]{:S(2)}) async-start(bf16[8,64,496]{2,1,0:T(8,128)(2,1)} %broadcast_in_dim.11), calls=%async_computation.6 | async-start | bytes 1048576 | tf_op jit(solution)/shard_map/all_to_all | solution.py:21
Sparse Core Ops, SparseCore 0:
  10.1 63.7 all-gather.2

commit v5 on v4

--- a/solution.py
+++ b/solution.py
@@ -14,7 +14,7 @@
 F32 = jnp.float32
 HIGHEST = lax.Precision.HIGHEST
 GRANT = 16 * 1024 * 1024
-WIDE_GRANT = 60 * 1024 * 1024
+WIDE_GRANT = 50 * 1024 * 1024
 
 
 def exchange(pieces, axes):
@@ -169,21 +169,33 @@
     done = []
     for k in range(0, rank, 2):
         first, second = work[k : k + 1, :], work[k + 1 : k + 2, :]
-        left, right = work[:, k : k + 1], work[:, k + 1 : k + 2]
-        root = lax.rsqrt(first[:, k : k + 1])
-        first, left = first * root, left * root
-        cross = first[:, k + 1 : k + 2]
-        root = lax.rsqrt(second[:, k + 1 : k + 2] - cross * cross)
-        second = (second - cross * first) * root
-        right = (right - cross * left) * root
+        pivot = jnp.broadcast_to(first[:, k : k + 1], first.shape)
+        cross = jnp.broadcast_to(first[:, k + 1 : k + 2], first.shape)
+        pivot_2 = jnp.broadcast_to(second[:, k + 1 : k + 2], first.shape)
+        left = jnp.broadcast_to(work[:, k : k + 1], work.shape)
+        right = jnp.broadcast_to(work[:, k + 1 : k + 2], work.shape)
+        root = lax.rsqrt(pivot)
+        cross = cross * root
+        root_2 = lax.rsqrt(pivot_2 - cross * cross)
+        first = first * root
+        second = (second - cross * first) * root_2
         done.append(first[:, rank:])
         done.append(second[:, rank:])
         if k + 2 < rank:
             rest = below > k + 1
-            work = work - (
-                jnp.where(rest, left, 0.0) * first + jnp.where(rest, right, 0.0) * second
-            )
+            left = left * root
+            right = (right - cross * left) * root_2
+            change = left * first + right * second
+            work = jnp.where(rest, work - change, work)
     out_ref[...] = jnp.concatenate(done, axis=0)
+
+
+def own_body(inverse_ref, mixed_ref, own_ref, out_ref):
+    own = nn(inverse_ref[...], mixed_ref[...], precision=HIGHEST)
+    own_ref[...] = own
+    rounded = own.astype(BF16)
+    for i in range(out_ref.shape[0]):
+        out_ref[i] = rounded
 
 
 def residue_body(q_ref, p_ref, merged_ref, out_hbm, out_ref, sems):
@@ -276,9 +288,15 @@
 
     (inverse,) = local_call(inverse_body, [shaped((rank, rank), F32)], gram, flops=4 * rank**3)
     p_hat = nn(inverse, p_t, precision=HIGHEST)
-    q_own = nn(inverse, mixed, precision=HIGHEST)
-
-    q_parts = sent_to_all(q_own.astype(BF16), "mp")
+    q_own, q_copies = local_call(
+        own_body,
+        [shaped((rank, cols), F32), shaped((shards, rank, cols), BF16)],
+        inverse,
+        mixed,
+        flops=12 * rank * rank * cols,
+    )
+
+    q_parts = exchange(q_copies, "mp")
     new_error = residue(q_parts, p_hat.astype(BF16).T, merged)
     scale = jnp.sqrt(F32(rows * shards))
     return (new_error, (p_hat * scale).T, q_own.T)

time: 176 us -> 171 us (0.972)
  Pallas kernels: 15.2 us -> 11.8 us
  local copies, waits for them, and re-layouts: 6.84 us -> 3.74 us
  waiting for transfers between devices: 31.6 us -> 34.5 us
    all_to_all x3, waiting for transfers between devices: 30.9 us -> 33.8 us  [exchange(): return lax.all_to_all(pieces, axes, split_axis=0, concat_axis=0, tiled=True)]
    unnamed x14 -> x11, local copies, waits for them, and re-layouts: 4.35 us -> 2.1 us
    pallas_call x1, Pallas kernels: 6.18 us -> 3.93 us  [merge(): pl.pallas_call(merged_body, name='merged', out_shape=shaped((rows, width)...]
    pallas_call x6 -> x7, Pallas kernels: 7.35 us -> 6.28 us  [local_call(): pl.pallas_call(body, out_shape=list(outs), in_specs=[spec] * len(args), o...]
  transfers between devices with their start and end apart: 4 -> 4, of which waited for: 3 -> 3; matrix products, arithmetic and copies ran while one was open for 1% -> 1% of each run, Pallas kernels for 4% -> 3%
where the time goes in v5:
time: 171 us; the launch traced here: 170 us
  blocking collectives  89.9 us (53%)
  waiting for transfers between devices  34.5 us (20%)
  starting transfers between devices  15.2 us (9%)
  between operations  14.2 us (8%)
  Pallas kernels  11.8 us (7%)
  local copies, waits for them, and re-layouts  3.74 us (2%)
    all_to_all x4, blocking collectives, exchange(): return lax.all_to_all(pieces, axes, split_axis=0, concat_axis=0, tiled=True)  65.3 us
    all_to_all x3, waiting for transfers between devices, exchange(): return lax.all_to_all(pieces, axes, split_axis=0, concat_axis=0, tiled=True)  33.8 us
    all_gather x1, blocking collectives, layer(): first = lax.all_gather(packed, 'mp')  24.7 us
    all_to_all x3, starting transfers between devices, exchange(): return lax.all_to_all(pieces, axes, split_axis=0, concat_axis=0, tiled=True)  15.1 us
    pallas_call x7, Pallas kernels, local_call(): pl.pallas_call(body, out_shape=list(outs), in_specs=[spec] * len(args), o...  6.28 us
    pallas_call x1, Pallas kernels, merge(): pl.pallas_call(merged_body, name='merged', out_shape=shaped((rows, width)...  3.93 us
  transfers between devices with their start and end apart: 4, of which 3 were waited for; matrix products, arithmetic and copies ran while one was open for 1% of the time, Pallas kernels for 3%

profile of v5, /device:TPU:1, one launch (start us, length us, event | category | flops | bytes accessed | tf_op | source)
XLA Modules:
  0.0 170.4 jit_solution(2859643227592839953)
XLA Ops:
  7.2 0.7 all-gather.3.cloned.1.call-update
  7.9 1.0 copy-done.1
  8.9 0.9 copy-done.3
  9.9 0.3 shard_map.67
  10.1 24.7 %all-gather = bf16[512,1008]{1,0:T(8,128)(2,1)S(1)} all-gather(bf16[64,1008]{1,0:T(8,128)(2,1)S(1)} %shard_map.67), channel_id=2, replica_groups=mesh['dp_0'=4,'dp_1'=8,'dp_2'=2,'mp'=8] {'mp'}, dimensions={0}, use_global_device_ids=true | all-gather | bytes 1161216 | tf_op jit(solution)/shard_map/all_gather | solution.py:256
  34.8 0.8 shard_map.68
  35.7 31.1 %all_to_all.55 = f32[64,1,256]{2,1,0:T(1,128)S(1)} all-to-all(f32[64,1,256]{2,1,0:T(1,128)S(1)} %copy.13), channel_id=1, replica_groups=mesh['dp_0'=4,'dp_1'=8,'dp_2'=2,'mp'=8] {'dp_0','dp_1','dp_2'}, dimensions={0} | all-to-all | bytes 131072 | tf_op jit(solution)/shard_map/all_to_all | solution.py:21
  66.9 0.7 broadcast_in_dim.6
  67.6 4.4 %all-to-all-start.1 = ((f32[64,1,256]{2,1,0:T(1,128)}), f32[64,1,256]{2,1,0:T(1,128)S(1)}, u32[]{:S(2)}, u32[]{:S(2)}) async-start(f32[64,1,256]{2,1,0:T(1,128)} %broadcast_in_dim.6), calls=%async_computation.1 | async-start | bytes 131072 | tf_op jit(solution)/shard_map/all_to_all | solution.py:21
  72.2 9.7 %all-to-all-done.1 = f32[64,1,256]{2,1,0:T(1,128)S(1)} async-done(((f32[64,1,256]{2,1,0:T(1,128)}), f32[64,1,256]{2,1,0:T(1,128)S(1)}, u32[]{:S(2)}, u32[]{:S(2)}) %all-to-all-start.1) | async-done | bytes 65568 | tf_op jit(solution)/shard_map/all_to_all | solution.py:21
  81.9 3.9 %merged.1.merged_ref = bf16[256,3968]{1,0:T(8,128)(2,1)S(1)} custom-call(bf16[256,512]{1,0:T(8,128)(2,1)S(1)} %bitcast.23, bf16[256,3968]{1,0:T(8,128)(2,1)} %e_hbm.1, bf16[3968,512]{1,0:T(8,128)(2,1)} %all-gather.3.cloned.1.call-done.x_hbm), custom_call_target="tpu_custom_call" | custom-call | flops 1040187392 | bytes 8126464 | tf_op jit(solution)/shard_map/merged/pallas_call | solution.py:97
  85.9 0.5 shard_map.69
  86.4 4.2 %all_to_all.56 = bf16[2,32,3968]{2,1,0:T(8,128)(2,1)S(1)} all-to-all(bf16[2,32,3968]{2,1,0:T(8,128)(2,1)S(1)} %bitcast.25), channel_id=1, replica_groups=mesh['dp_0'=4,'dp_1'=8,'dp_2'=2,'mp'=8] {'dp_2'}, dimensions={0} | all-to-all | bytes 1015808 | tf_op jit(solution)/shard_map/all_to_all | solution.py:21
  90.7 18.1 %all_to_all.57.second_ref = bf16[8,32,752]{2,1,0:T(8,128)(2,1)S(1)} all-to-all(bf16[8,32,752]{2,1,0:T(8,128)(2,1)S(1)} %shard_map.70), channel_id=1, replica_groups=mesh['dp_0'=4,'dp_1'=8,'dp_2'=2,'mp'=8] {'mp'}, dimensions={0} | all-to-all | bytes 770048 | tf_op jit(solution)/shard_map/all_to_all | solution.py:21
  109.0 11.9 %all_to_all.58 = f32[32,1,496]{2,1,0:T(1,128)S(1)} all-to-all(f32[32,1,496]{2,1,0:T(1,128)S(1)} %copy.15), channel_id=1, replica_groups=mesh['dp_0'=4,'dp_1'=8,'dp_2'=2,'mp'=8] {'dp_0','dp_1'}, dimensions={0} | all-to-all | bytes 126976 | tf_op jit(solution)/shard_map/all_to_all | solution.py:21
  121.0 0.7 broadcast_in_dim.7
  121.7 7.2 %all-to-all-start.5 = ((f32[64,1,496]{2,1,0:T(1,128)}), f32[64,1,496]{2,1,0:T(1,128)S(1)}, u32[]{:S(2)}, u32[]{:S(2)}) async-start(f32[64,1,496]{2,1,0:T(1,128)} %broadcast_in_dim.7), calls=%async_computation.5 | async-start | bytes 262144 | tf_op jit(solution)/shard_map/all_to_all | solution.py:21
  128.9 3.3 %shard_map.72.inverse_ref = f32[64,64]{1,0:T(8,128)S(1)} custom-call(f32[64,64]{1,0:T(8,128)S(1)} %get-tuple-element.11.gram_ref), custom_call_target="tpu_custom_call" | custom-call | flops 1048576 | bytes 32768 | tf_op jit(solution)/shard_map/pallas_call | solution.py:39
  132.2 7.1 %all-to-all-done.5 = f32[64,1,496]{2,1,0:T(1,128)S(1)} async-done(((f32[64,1,496]{2,1,0:T(1,128)}), f32[64,1,496]{2,1,0:T(1,128)S(1)}, u32[]{:S(2)}, u32[]{:S(2)}) %all-to-all-start.5) | async-done | bytes 127008 | tf_op jit(solution)/shard_map/all_to_all | solution.py:21
  139.4 1.1 shard_map.73
  140.5 3.5 %all-to-all-start.6 = ((bf16[8,64,496]{2,1,0:T(8,128)(2,1)}), bf16[8,64,496]{2,1,0:T(8,128)(2,1)S(1)}, u32[]{:S(2)}, u32[]{:S(2)}) async-start(bf16[8,64,496]{2,1,0:T(8,128)(2,1)} %get-tuple-element.13), calls=%async_computation.6 | async-start | bytes 1048576 | tf_op jit(solution)/shard_map/all_to_all | solution.py:21
  144.0 0.8 broadcast_multiply_fusion
  144.9 16.9 %all-to-all-done.6.q_ref = bf16[8,64,496]{2,1,0:T(8,128)(2,1)S(1)} async-done(((bf16[8,64,496]{2,1,0:T(8,128)(2,1)}), bf16[8,64,496]{2,1,0:T(8,128)(2,1)S(1)}, u32[]{:S(2)}, u32[]{:S(2)}) %all-to-all-start.6) | async-done | bytes 507936 | tf_op jit(solution)/shard_map/all_to_all | solution.py:21
  161.9 1.6 residue.1
  (20 shorter events, 0.9 us)
Async XLA Ops:
  7.2 27.7 %copy-start = (bf16[256,3968]{1,0:T(8,128)(2,1)S(1)}, bf16[256,3968]{1,0:T(8,128)(2,1)}, u32[]{:S(2)}) copy-start(bf16[256,3968]{1,0:T(8,128)(2,1)} %e_hbm.1) | copy-start | bytes 6094852
  7.2 74.8 %all-gather.3.cloned.1.call-start = ((), (), s32[]{:S(2)}) async-start(), calls=%async_computation.7 | async-start | bytes 4571136 | tf_op jit(solution)/shard_map/all_gather | solution.py:247
  7.9 1.0 copy-start.1
  8.9 0.9 copy-start.3
  9.9 25.0 %copy-start.2 = (bf16[512,256]{1,0:T(8,128)(2,1)S(1)}, bf16[512,256]{1,0:T(8,128)(2,1)}, u32[]{:S(2)}) copy-start(bf16[512,256]{1,0:T(8,128)(2,1)} %g_ref.1) | copy-start | bytes 786436
  67.6 14.3 %all-to-all-start.1 = ((f32[64,1,256]{2,1,0:T(1,128)}), f32[64,1,256]{2,1,0:T(1,128)S(1)}, u32[]{:S(2)}, u32[]{:S(2)}) async-start(f32[64,1,256]{2,1,0:T(1,128)} %broadcast_in_dim.6), calls=%async_computation.1 | async-start | bytes 131072 | tf_op jit(solution)/shard_map/all_to_all | solution.py:21
  121.7 17.7 %all-to-all-start.5 = ((f32[64,1,496]{2,1,0:T(1,128)}), f32[64,1,496]{2,1,0:T(1,128)S(1)}, u32[]{:S(2)}, u32[]{:S(2)}) async-start(f32[64,1,496]{2,1,0:T(1,128)} %broadcast_in_dim.7), calls=%async_computation.5 | async-start | bytes 262144 | tf_op jit(solution)/shard_map/all_to_all | solution.py:21
  140.5 21.4 %all-to-all-start.6 = ((bf16[8,64,496]{2,1,0:T(8,128)(2,1)}), bf16[8,64,496]{2,1,0:T(8,128)(2,1)S(1)}, u32[]{:S(2)}, u32[]{:S(2)}) async-start(bf16[8,64,496]{2,1,0:T(8,128)(2,1)} %get-tuple-element.13), calls=%async_computation.6 | async-start | bytes 1048576 | tf_op jit(solution)/shard_map/all_to_all | solution.py:21
Sparse Core Ops, SparseCore 0:
  10.1 63.7 all-gather.2

commit v6 on v5

--- a/solution.py
+++ b/solution.py
@@ -1,3 +1,5 @@
+import functools
+
 import jax
 import jax.numpy as jnp
 from jax import lax
@@ -7,8 +9,6 @@
 from jax.sharding import PartitionSpec as P
 
 DP = ("dp_0", "dp_1", "dp_2")
-CHIPS = ("dp_0", "dp_1")
-CORE = "dp_2"
 DP_MP = ("dp_0", "dp_1", "dp_2", "mp")
 BF16 = jnp.bfloat16
 F32 = jnp.float32
@@ -120,40 +120,45 @@
 
 def product_body(p_ref, merged_ref, out_ref, gram_ref):
     rank = p_ref.shape[0]
+    width = merged_ref.shape[1]
+    half = out_ref.shape[0]
     p = p_ref[...]
-    gram = nt(p, p, precision=HIGHEST)
-    high = gram.astype(BF16)
-    gram_ref[:, :rank] = high
-    gram_ref[:, rank:] = (gram - high.astype(F32)).astype(BF16)
-    row = lax.broadcasted_iota(jnp.int32, (rank, rank), 0)
-    col = lax.broadcasted_iota(jnp.int32, (rank, rank), 1)
-    near = rank // 2
-    evens_first = jnp.where(row < near, 2 * row, 2 * (row - near) + 1)
-    p_b = nn((col == evens_first).astype(BF16), p.astype(BF16)).astype(BF16)
-    for lo, hi in column_tiles(merged_ref.shape[1]):
-        out_ref[:, lo:hi] = nn(p_b, merged_ref[:, lo:hi]).astype(BF16)
-
-
-def pack_body(pair_ref, gram_ref, out_ref):
-    _, width = gram_ref.shape
-    shards, near, size = out_ref.shape
-    both = jnp.concatenate([gram_ref[:near, :], gram_ref[near:, :]], axis=1)
-    summed = (pair_ref[:near, :].astype(F32) + pair_ref[near:, :].astype(F32)).astype(BF16)
-    cols = size - 2 * width
+    gram_ref[...] = nt(p, p, precision=HIGHEST)
+    p_b = p.astype(BF16)
+    for lo, hi in column_tiles(half):
+        left = nn(p_b, merged_ref[:, lo:hi])
+        end = min(half + hi, width)
+        right = nn(p_b, merged_ref[:, half + lo : end])
+        spare = half + hi - end
+        if spare:
+            right = jnp.concatenate([right, jnp.zeros((rank, spare), F32)], axis=1)
+        out_ref[lo:hi, :] = jnp.concatenate([left, right], axis=0).T.astype(BF16)
+
+
+def spread_body(arrived_ref, gram_ref, out_ref):
+    shards, size, _ = out_ref.shape
+    near = size // 2
+    total = arrived_ref[:near, :].astype(F32)
+    for i in range(1, arrived_ref.shape[0] // near):
+        total = total + arrived_ref[i * near : (i + 1) * near, :].astype(F32)
+    rank = gram_ref.shape[0]
+    gram = jnp.concatenate([gram_ref[: rank // 2, :], gram_ref[rank // 2 :, :]], axis=1)
     for i in range(shards):
-        out_ref[i, :, : 2 * width] = both
-        out_ref[i, :, 2 * width :] = summed[:, i * cols : (i + 1) * cols]
-
-
-def total_body(second_ref, out_ref, gram_ref):
-    near = out_ref.shape[0]
+        out_ref[i, :near, :] = total
+        out_ref[i, near:, :] = gram
+
+
+def settle_body(second_ref, out_ref, gram_ref, *, replicas):
+    near = second_ref.shape[1] // 2
     rank = gram_ref.shape[0]
-    total = second_ref[0].astype(F32)
+    total = second_ref[0]
     for i in range(1, second_ref.shape[0]):
-        total = total + second_ref[i].astype(F32)
-    gram_ref[:near, :] = total[:, :rank] + total[:, rank : 2 * rank]
-    gram_ref[near:, :] = total[:, 2 * rank : 3 * rank] + total[:, 3 * rank : 4 * rank]
-    out_ref[...] = total[:, 4 * rank :]
+        total = total + second_ref[i]
+    gram_ref[: rank // 2, :] = total[near:, :rank]
+    gram_ref[rank // 2 :, :] = total[near:, rank:]
+    rounded = (total[:near, :] / replicas).astype(BF16)
+    for i in range(out_ref.shape[0] // near):
+        out_ref[i * near : (i + 1) * near, :] = rounded
 
 
 def inverse_body(gram_ref, out_ref):
@@ -190,42 +195,72 @@
     out_ref[...] = jnp.concatenate(done, axis=0)
 
 
-def own_body(inverse_ref, mixed_ref, own_ref, out_ref):
-    own = nn(inverse_ref[...], mixed_ref[...], precision=HIGHEST)
-    own_ref[...] = own
-    rounded = own.astype(BF16)
-    for i in range(out_ref.shape[0]):
-        out_ref[i] = rounded
-
-
-def residue_body(q_ref, p_ref, merged_ref, out_hbm, out_ref, sems):
-    shards = q_ref.shape[0]
-    q_full = jnp.concatenate([q_ref[i] for i in range(shards)], axis=1)
+def residue_body(
+    shard_ref, packed_ref, inverse_ref, p_ref, merged_ref, out_hbm, own_ref, out_ref, sems
+):
+    rank, cols = own_ref.shape
+    half = packed_ref.shape[0]
+    width = merged_ref.shape[1]
+    inverse = inverse_ref[...]
+    high = inverse.astype(BF16)
+    low = (inverse - high.astype(F32)).astype(BF16)
+    none = jnp.zeros((rank, rank), F32)
+    twice = jnp.concatenate(
+        [jnp.concatenate([inverse.T, none], axis=1), jnp.concatenate([none, inverse.T], axis=1)],
+        axis=0,
+    )
+    twice_high = twice.astype(BF16)
+    twice_low = (twice - twice_high.astype(F32)).astype(BF16)
     p_rows = p_ref[...]
+    no_rows = jnp.zeros(p_rows.shape, BF16)
+    sides = [
+        (0, jnp.concatenate([p_rows, no_rows], axis=1)),
+        (half, jnp.concatenate([no_rows, p_rows], axis=1)),
+    ]
     copies = []
-    for i, (lo, hi) in enumerate(column_tiles(merged_ref.shape[1])):
-        approx = nn(p_rows, q_full[:, lo:hi])
-        out_ref[:, lo:hi] = (merged_ref[:, lo:hi].astype(F32) - approx).astype(BF16)
-        copies.append(
-            pltpu.make_async_copy(out_ref.at[:, lo:hi], out_hbm.at[:, lo:hi], sems.at[i])
-        )
-        copies[-1].start()
+    for lo, hi in column_tiles(half):
+        packed = packed_ref[lo:hi, :]
+        q = (nn(packed, twice_high) + nn(packed, twice_low)).astype(BF16)
+        for start, rows in sides:
+            first, last = start + lo, min(start + hi, width)
+            approx = nt(rows, q)[:, : last - first]
+            made = merged_ref[:, first:last].astype(F32) - approx
+            out_ref[:, first:last] = made.astype(BF16)
+            copies.append(
+                pltpu.make_async_copy(
+                    out_ref.at[:, first:last], out_hbm.at[:, first:last], sems.at[len(copies)]
+                )
+            )
+            copies[-1].start()
+    for i in range(width // cols):
+
+        @pl.when(shard_ref[0] == i)
+        def _():
+            first, last = i * cols, (i + 1) * cols
+            parts = []
+            if first < half:
+                parts.append(packed_ref[first : min(last, half), :rank])
+            if last > half:
+                parts.append(packed_ref[max(first, half) - half : last - half, rank:])
+            mine = parts[0] if len(parts) == 1 else jnp.concatenate(parts, axis=0)
+            own_ref[...] = nt(high, mine) + nt(low, mine)
+
     for copy in copies:
         copy.wait()
 
 
-def residue(q_parts, p_rows, merged):
+def residue(shard, packed, inverse, p_rows, merged, cols):
     rows, width = merged.shape
     spec = pl.BlockSpec(memory_space=pltpu.VMEM)
     return pl.pallas_call(
         residue_body,
         name="residue",
-        out_shape=shaped((rows, width), BF16),
-        in_specs=[spec] * 3,
-        out_specs=pl.BlockSpec(memory_space=pltpu.HBM),
+        out_shape=[shaped((rows, width), BF16), shaped((inverse.shape[0], cols), F32)],
+        in_specs=[pl.BlockSpec(memory_space=pltpu.SMEM), spec, spec, spec, spec],
+        out_specs=[pl.BlockSpec(memory_space=pltpu.HBM), spec],
         scratch_shapes=[
             pltpu.VMEM((rows, width), BF16),
-            pltpu.SemaphoreType.DMA((len(column_tiles(width)),)),
+            pltpu.SemaphoreType.DMA((2 * len(column_tiles(packed.shape[0])),)),
         ],
         compiler_params=pltpu.CompilerParams(vmem_limit_bytes=GRANT),
         cost_estimate=pl.CostEstimate(
@@ -233,7 +268,7 @@
             bytes_accessed=4 * rows * width,
             transcendentals=0,
         ),
-    )(q_parts, p_rows, merged)
+    )(shard, packed, inverse, p_rows, merged)
 
 
 def layer(inputs, grad_out, error, q_prev):
@@ -246,14 +281,14 @@
     x_t = inputs.T
     x_full = lax.all_gather(x_t, "mp", axis=0, tiled=True)
 
-    (packed,) = local_call(
+    (sent,) = local_call(
         start_body,
         [shaped((rank, tokens + cols), BF16)],
         x_t,
         q_prev.T,
         flops=4 * rank * tokens * cols,
     )
-    first = lax.all_gather(packed, "mp")
+    first = lax.all_gather(sent, "mp")
     (p_part,) = local_call(
         p_body,
         [shaped((rank, rows), F32)],
@@ -266,38 +301,27 @@
     p_t = sent_to_all(p_row, DP)
 
     merged = merge(grad_out.T, error, x_full)
+    near = -(-width // (2 * replicas * 16)) * 16
     product, gram_part = local_call(
         product_body,
-        [shaped((rank, width), BF16), shaped((rank, 2 * rank), BF16)],
+        [shaped((replicas * near, 2 * rank), BF16), shaped((rank, rank), F32)],
         p_t,
         merged,
         flops=2 * rows * width * rank,
     )
-    near = rank // lax.axis_size(CORE)
     (pieces,) = local_call(
-        pack_body,
-        [shaped((shards, near, 4 * rank + cols), BF16)],
-        exchange(product, CORE),
-        gram_part,
-    )
-    q_part, gram = local_call(
-        total_body, [shaped((near, cols), F32), shaped((rank, rank), F32)], exchange(pieces, "mp")
-    )
-    q_row = jnp.sum(exchange(q_part, CHIPS), axis=0) / replicas
-    mixed = sent_to_all(q_row, DP)
-
+        spread_body, [shaped((shards, 2 * near, 2 * rank), F32)], exchange(product, DP), gram_part
+    )
+    q_copies, gram = local_call(
+        functools.partial(settle_body, replicas=replicas),
+        [shaped(product.shape, BF16), shaped((rank, rank), F32)],
+        exchange(pieces, "mp"),
+    )
+    packed = exchange(q_copies, DP)
     (inverse,) = local_call(inverse_body, [shaped((rank, rank), F32)], gram, flops=4 * rank**3)
     p_hat = nn(inverse, p_t, precision=HIGHEST)
-    q_own, q_copies = local_call(
-        own_body,
-        [shaped((rank, cols), F32), shaped((shards, rank, cols), BF16)],
-        inverse,
-        mixed,
-        flops=12 * rank * rank * cols,
-    )
-
-    q_parts = exchange(q_copies, "mp")
-    new_error = residue(q_parts, p_hat.astype(BF16).T, merged)
+    shard = lax.axis_index("mp").astype(jnp.int32).reshape(1)
+    new_error, q_own = residue(shard, packed, inverse, p_hat.astype(BF16).T, merged, cols)
     scale = jnp.sqrt(F32(rows * shards))
     return (new_error, (p_hat * scale).T, q_own.T)
 

time: 171 us -> 159 us (0.930)
  waiting for transfers between devices: 34.5 us -> 23.4 us
  starting transfers between devices: 15.2 us -> 10.8 us
  blocking collectives: 89.9 us -> 93.3 us
    all_to_all x3 -> x2, waiting for transfers between devices: 33.8 us -> 22.8 us  [exchange(): return lax.all_to_all(pieces, axes, split_axis=0, concat_axis=0, tiled=True)]
    all_to_all x3 -> x2, starting transfers between devices: 15.1 us -> 10.7 us  [exchange(): return lax.all_to_all(pieces, axes, split_axis=0, concat_axis=0, tiled=True)]
    all_to_all x4 -> x3, blocking collectives: 65.3 us -> 68.6 us  [exchange(): return lax.all_to_all(pieces, axes, split_axis=0, concat_axis=0, tiled=True)]
    pallas_call x7 -> x6, Pallas kernels: 6.28 us -> 5.92 us  [local_call(): pl.pallas_call(body, out_shape=list(outs), in_specs=[spec] * len(args), o...]
  transfers between devices with their start and end apart: 4 -> 3, of which waited for: 3 -> 2; matrix products, arithmetic and copies ran while one was open for 1% -> 1% of each run, Pallas kernels for 3% -> 3%
where the time goes in v6:
time: 159 us
  blocking collectives  93.3 us (59%)
  waiting for transfers between devices  23.4 us (15%)
  between operations  14.1 us (9%)
  Pallas kernels  13 us (8%)
  starting transfers between devices  10.8 us (7%)
  local copies, waits for them, and re-layouts  2.94 us (2%)
    all_to_all x3, blocking collectives, exchange(): return lax.all_to_all(pieces, axes, split_axis=0, concat_axis=0, tiled=True)  68.6 us
    all_gather x1, blocking collectives, layer(): first = lax.all_gather(sent, 'mp')  24.7 us
    all_to_all x2, waiting for transfers between devices, exchange(): return lax.all_to_all(pieces, axes, split_axis=0, concat_axis=0, tiled=True)  22.8 us
    all_to_all x2, starting transfers between devices, exchange(): return lax.all_to_all(pieces, axes, split_axis=0, concat_axis=0, tiled=True)  10.7 us
    pallas_call x6, Pallas kernels, local_call(): pl.pallas_call(body, out_shape=list(outs), in_specs=[spec] * len(args), o...  5.92 us
    pallas_call x1, Pallas kernels, merge(): pl.pallas_call(merged_body, name='merged', out_shape=shaped((rows, width)...  3.93 us
  transfers between devices with their start and end apart: 3, of which 2 were waited for; matrix products, arithmetic and copies ran while one was open for 1% of the time, Pallas kernels for 3%

profile of v6, /device:TPU:1, one launch (start us, length us, event | category | flops | bytes accessed | tf_op | source)
XLA Modules:
  0.0 158.5 jit_solution(10148583991688992467)
XLA Ops:
  7.2 0.7 all-gather.3.cloned.1.call-update
  7.9 1.0 copy-done.1
  8.9 0.9 copy-done.3
  9.9 0.3 shard_map.67
  10.1 24.7 %all-gather = bf16[512,1008]{1,0:T(8,128)(2,1)S(1)} all-gather(bf16[64,1008]{1,0:T(8,128)(2,1)S(1)} %shard_map.67), channel_id=2, replica_groups=mesh['dp_0'=4,'dp_1'=8,'dp_2'=2,'mp'=8] {'mp'}, dimensions={0}, use_global_device_ids=true | all-gather | bytes 1161216 | tf_op jit(solution)/shard_map/all_gather | solution.py:291
  34.8 0.8 shard_map.68
  35.7 31.1 %all_to_all.44 = f32[64,1,256]{2,1,0:T(1,128)S(1)} all-to-all(f32[64,1,256]{2,1,0:T(1,128)S(1)} %copy.12), channel_id=1, replica_groups=mesh['dp_0'=4,'dp_1'=8,'dp_2'=2,'mp'=8] {'dp_0','dp_1','dp_2'}, dimensions={0} | all-to-all | bytes 131072 | tf_op jit(solution)/shard_map/all_to_all | solution.py:21
  66.8 0.1 reduce_sum.9
  66.9 0.7 broadcast_in_dim.3
  67.6 4.4 %all-to-all-start.1 = ((f32[64,1,256]{2,1,0:T(1,128)}), f32[64,1,256]{2,1,0:T(1,128)S(1)}, u32[]{:S(2)}, u32[]{:S(2)}) async-start(f32[64,1,256]{2,1,0:T(1,128)} %broadcast_in_dim.3), calls=%async_computation.1 | async-start | bytes 131072 | tf_op jit(solution)/shard_map/all_to_all | solution.py:21
  72.0 0.1 copy.13
  72.2 9.7 %all-to-all-done.1 = f32[64,1,256]{2,1,0:T(1,128)S(1)} async-done(((f32[64,1,256]{2,1,0:T(1,128)}), f32[64,1,256]{2,1,0:T(1,128)S(1)}, u32[]{:S(2)}, u32[]{:S(2)}) %all-to-all-start.1) | async-done | bytes 65568 | tf_op jit(solution)/shard_map/all_to_all | solution.py:21
  81.9 3.9 %merged.1.merged_ref = bf16[256,3968]{1,0:T(8,128)(2,1)S(1)} custom-call(bf16[256,512]{1,0:T(8,128)(2,1)S(1)} %bitcast.23, bf16[256,3968]{1,0:T(8,128)(2,1)} %e_hbm.1, bf16[3968,512]{1,0:T(8,128)(2,1)} %all-gather.3.cloned.1.call-done.x_hbm), custom_call_target="tpu_custom_call" | custom-call | flops 1040187392 | bytes 8126464 | tf_op jit(solution)/shard_map/merged/pallas_call | solution.py:97
  85.9 0.6 shard_map.69
  86.5 21.1 %all_to_all.45 = bf16[64,32,128]{2,1,0:T(8,128)(2,1)S(1)} all-to-all(bf16[64,32,128]{2,1,0:T(8,128)(2,1)S(1)} %bitcast.24), channel_id=1, replica_groups=mesh['dp_0'=4,'dp_1'=8,'dp_2'=2,'mp'=8] {'dp_0','dp_1','dp_2'}, dimensions={0} | all-to-all | bytes 1048576 | tf_op jit(solution)/shard_map/all_to_all | solution.py:21
  107.6 0.1 shard_map.70
  107.7 16.4 %all_to_all.46.second_ref = f32[8,64,128]{2,1,0:T(8,128)S(1)} all-to-all(f32[8,64,128]{2,1,0:T(8,128)S(1)} %shard_map.70), channel_id=1, replica_groups=mesh['dp_0'=4,'dp_1'=8,'dp_2'=2,'mp'=8] {'mp'}, dimensions={0} | all-to-all | bytes 524288 | tf_op jit(solution)/shard_map/all_to_all | solution.py:21
  124.1 0.8 shard_map.71
  125.0 6.3 %all-to-all-start.4 = ((bf16[64,32,128]{2,1,0:T(8,128)(2,1)}), bf16[64,32,128]{2,1,0:T(8,128)(2,1)S(1)}, u32[]{:S(2)}, u32[]{:S(2)}) async-start(bf16[64,32,128]{2,1,0:T(8,128)(2,1)} %bitcast.8), calls=%async_computation.4 | async-start | bytes 1048576 | tf_op jit(solution)/shard_map/all_to_all | solution.py:21
  131.2 3.3 %shard_map.72.inverse_ref = f32[64,64]{1,0:T(8,128)S(1)} custom-call(f32[64,64]{1,0:T(8,128)S(1)} %get-tuple-element.12.gram_ref), custom_call_target="tpu_custom_call" | custom-call | flops 1048576 | bytes 32768 | tf_op jit(solution)/shard_map/pallas_call | solution.py:39
  134.5 0.9 broadcast_multiply_fusion
  135.4 0.1 copy.14.p_ref
  135.5 13.0 %all-to-all-done.4 = bf16[64,32,128]{2,1,0:T(8,128)(2,1)S(1)} async-done(((bf16[64,32,128]{2,1,0:T(8,128)(2,1)}), bf16[64,32,128]{2,1,0:T(8,128)(2,1)S(1)}, u32[]{:S(2)}, u32[]{:S(2)}) %all-to-all-start.4) | async-done | bytes 524320 | tf_op jit(solution)/shard_map/all_to_all | solution.py:21
  148.5 3.1 %residue.1 = (bf16[256,3968]{1,0:T(8,128)(2,1)}, f32[64,496]{1,0:T(8,128)}) custom-call(s32[1]{0:T(128)} %bitcast.shard_ref, bf16[2048,128]{1,0:T(8,128)(2,1)S(1)} %bitcast.20, f32[64,64]{1,0:T(8,128)S(1)} %shard_map.72.inverse_ref, bf16[256,64]{1,0:T(8,128)(2,1)S(1)} %copy.14.p_ref, bf16[256,3968]{1,0:T(8,128)(2,1)S(1)} %merged.1.merged_ref), custom_call_target="tpu_custom_call" | custom-call | flops 130023424 | bytes 4063232 | tf_op jit(solution)/shard_map/residue/pallas_call | solution.py:255
  (11 shorter events, 0.1 us)
Async XLA Ops:
  7.2 27.7 %copy-start = (bf16[256,3968]{1,0:T(8,128)(2,1)S(1)}, bf16[256,3968]{1,0:T(8,128)(2,1)}, u32[]{:S(2)}) copy-start(bf16[256,3968]{1,0:T(8,128)(2,1)} %e_hbm.1) | copy-start | bytes 6094852
  7.2 74.8 %all-gather.3.cloned.1.call-start = ((), (), s32[]{:S(2)}) async-start(), calls=%async_computation.5 | async-start | bytes 4571136 | tf_op jit(solution)/shard_map/all_gather | solution.py:282
  7.9 1.0 copy-start.1
  8.9 0.9 copy-start.3
  9.9 25.0 %copy-start.2 = (bf16[512,256]{1,0:T(8,128)(2,1)S(1)}, bf16[512,256]{1,0:T(8,128)(2,1)}, u32[]{:S(2)}) copy-start(bf16[512,256]{1,0:T(8,128)(2,1)} %g_ref.1) | copy-start | bytes 786436
  67.6 14.3 %all-to-all-start.1 = ((f32[64,1,256]{2,1,0:T(1,128)}), f32[64,1,256]{2,1,0:T(1,128)S(1)}, u32[]{:S(2)}, u32[]{:S(2)}) async-start(f32[64,1,256]{2,1,0:T(1,128)} %broadcast_in_dim.3), calls=%async_computation.1 | async-start | bytes 131072 | tf_op jit(solution)/shard_map/all_to_all | solution.py:21
  125.0 23.6 %all-to-all-start.4 = ((bf16[64,32,128]{2,1,0:T(8,128)(2,1)}), bf16[64,32,128]{2,1,0:T(8,128)(2,1)S(1)}, u32[]{:S(2)}, u32[]{:S(2)}) async-start(bf16[64,32,128]{2,1,0:T(8,128)(2,1)} %bitcast.8), calls=%async_computation.4 | async-start | bytes 1048576 | tf_op jit(solution)/shard_map/all_to_all | solution.py:21
Sparse Core Ops, SparseCore 0:
  10.1 63.7 all-gather.2

commit v7 on v6

--- a/solution.py
+++ b/solution.py
@@ -15,6 +15,7 @@
 HIGHEST = lax.Precision.HIGHEST
 GRANT = 16 * 1024 * 1024
 WIDE_GRANT = 50 * 1024 * 1024
+START_GRANT = 55000 * 1024
 
 
 def exchange(pieces, axes):
@@ -50,14 +51,41 @@
     return jax.ShapeDtypeStruct(shape, dtype)
 
 
-def start_body(x_ref, q_ref, out_ref):
+def start_body(x_hbm, q_hbm, out_ref, x_ref, q_ref, sems):
     tokens = x_ref.shape[1]
+    x_copy = pltpu.make_async_copy(x_hbm, x_ref, sems.at[0])
+    q_copy = pltpu.make_async_copy(q_hbm, q_ref, sems.at[1])
+    x_copy.start()
+    q_copy.start()
+    q_copy.wait()
     q = q_ref[...]
     high = q.astype(BF16)
     low = (q - high.astype(F32)).astype(BF16)
+    out_ref[:, tokens:] = high
+    x_copy.wait()
     x = x_ref[...]
     out_ref[:, :tokens] = (nn(high, x) + nn(low, x)).astype(BF16)
-    out_ref[:, tokens:] = high
+
+
+def started(x_t, q_t):
+    cols, tokens = x_t.shape
+    rank = q_t.shape[0]
+    return pl.pallas_call(
+        start_body,
+        name="start",
+        out_shape=shaped((rank, tokens + cols), BF16),
+        in_specs=[pl.BlockSpec(memory_space=pltpu.HBM)] * 2,
+        out_specs=pl.BlockSpec(memory_space=pltpu.VMEM),
+        scratch_shapes=[
+            pltpu.VMEM(x_t.shape, x_t.dtype),
+            pltpu.VMEM(q_t.shape, q_t.dtype),
+            pltpu.SemaphoreType.DMA((2,)),
+        ],
+        compiler_params=pltpu.CompilerParams(vmem_limit_bytes=START_GRANT),
+        cost_estimate=pl.CostEstimate(
+            flops=4 * rank * tokens * cols, bytes_accessed=2 * tokens * cols, transcendentals=0
+        ),
+    )(x_t, q_t)
 
 
 def p_body(first_ref, g_ref, e_ref, out_ref):
@@ -137,26 +165,30 @@
 
 def spread_body(arrived_ref, gram_ref, out_ref):
     shards, size, _ = out_ref.shape
-    near = size // 2
+    rank = gram_ref.shape[0]
+    near = size - rank
     total = arrived_ref[:near, :].astype(F32)
     for i in range(1, arrived_ref.shape[0] // near):
         total = total + arrived_ref[i * near : (i + 1) * near, :].astype(F32)
+    gram = jnp.concatenate([gram_ref[: rank // 2, :], gram_ref[rank // 2 :, :]], axis=1)
+    high = gram.astype(BF16)
+    low = (gram - high.astype(F32)).astype(BF16)
+    block = jnp.concatenate([high, low, total.astype(BF16)], axis=0)
+    for i in range(shards):
+        out_ref[i] = block
+
+
+def settle_body(second_ref, out_ref, gram_ref, *, replicas):
     rank = gram_ref.shape[0]
-    gram = jnp.concatenate([gram_ref[: rank // 2, :], gram_ref[rank // 2 :, :]], axis=1)
-    for i in range(shards):
-        out_ref[i, :near, :] = total
-        out_ref[i, near:, :] = gram
-
-
-def settle_body(second_ref, out_ref, gram_ref, *, replicas):
-    near = second_ref.shape[1] // 2
-    rank = gram_ref.shape[0]
-    total = second_ref[0]
+    near = second_ref.shape[1] - rank
+    half = rank // 2
+    total = second_ref[0].astype(F32)
     for i in range(1, second_ref.shape[0]):
-        total = total + second_ref[i]
-    gram_ref[: rank // 2, :] = total[near:, :rank]
-    gram_ref[rank // 2 :, :] = total[near:, rank:]
-    rounded = (total[:near, :] / replicas).astype(BF16)
+        total = total + second_ref[i].astype(F32)
+    gram = total[:half, :] + total[half:rank, :]
+    gram_ref[:half, :] = gram[:, :rank]
+    gram_ref[half:, :] = gram[:, rank:]
+    rounded = (total[rank:, :] / replicas).astype(BF16)
     for i in range(out_ref.shape[0] // near):
         out_ref[i * near : (i + 1) * near, :] = rounded
 
@@ -281,13 +313,7 @@
     x_t = inputs.T
     x_full = lax.all_gather(x_t, "mp", axis=0, tiled=True)
 
-    (sent,) = local_call(
-        start_body,
-        [shaped((rank, tokens + cols), BF16)],
-        x_t,
-        q_prev.T,
-        flops=4 * rank * tokens * cols,
-    )
+    sent = started(x_t, q_prev.T)
     first = lax.all_gather(sent, "mp")
     (p_part,) = local_call(
         p_body,
@@ -310,7 +336,10 @@
         flops=2 * rows * width * rank,
     )
     (pieces,) = local_call(
-        spread_body, [shaped((shards, 2 * near, 2 * rank), F32)], exchange(product, DP), gram_part
+        spread_body,
+        [shaped((shards, rank + near, 2 * rank), BF16)],
+        exchange(product, DP),
+        gram_part,
     )
     q_copies, gram = local_call(
         functools.partial(settle_body, replicas=replicas),

time: 159 us -> 157 us (0.987)
  blocking collectives: 93.3 us -> 91.1 us
  local copies, waits for them, and re-layouts: 2.94 us -> 1.01 us
    unnamed x10 -> x6, local copies, waits for them, and re-layouts: 2.09 us -> 0.16 us
    all_to_all x3, blocking collectives: 68.6 us -> 66.9 us  [exchange(): return lax.all_to_all(pieces, axes, split_axis=0, concat_axis=0, tiled=True)]
    pallas_call x6 -> x5, Pallas kernels: 5.92 us -> 5.64 us  [local_call(): pl.pallas_call(body, out_shape=list(outs), in_specs=[spec] * len(args), o...]
where the time goes in v7:
time: 157 us
  blocking collectives  91.1 us (58%)
  waiting for transfers between devices  23.4 us (15%)
  Pallas kernels  14.1 us (9%)
  between operations  14.1 us (9%)
  starting transfers between devices  11.9 us (8%)
    all_to_all x3, blocking collectives, exchange(): return lax.all_to_all(pieces, axes, split_axis=0, concat_axis=0, tiled=True)  66.9 us
    all_gather x1, blocking collectives, layer(): first = lax.all_gather(sent, 'mp')  24.2 us
    all_to_all x2, waiting for transfers between devices, exchange(): return lax.all_to_all(pieces, axes, split_axis=0, concat_axis=0, tiled=True)  22.7 us
    all_to_all x2, starting transfers between devices, exchange(): return lax.all_to_all(pieces, axes, split_axis=0, concat_axis=0, tiled=True)  11.8 us
    pallas_call x5, Pallas kernels, local_call(): pl.pallas_call(body, out_shape=list(outs), in_specs=[spec] * len(args), o...  5.64 us
    pallas_call x1, Pallas kernels, merge(): pl.pallas_call(merged_body, name='merged', out_shape=shaped((rows, width)...  3.94 us
  transfers between devices with their start and end apart: 3, of which 2 were waited for; matrix products, arithmetic and copies ran while one was open for 1% of the time, Pallas kernels for 3%

profile of v7, /device:TPU:1, one launch (start us, length us, event | category | flops | bytes accessed | tf_op | source)
XLA Modules:
  0.0 156.6 jit_solution(18316136024775136660)
XLA Ops:
  7.2 0.0 all-gather.3.cloned.1.call-start
  7.2 0.7 all-gather.3.cloned.1.call-update
  7.9 1.4 start.1
  9.3 24.2 %all-gather = bf16[512,1008]{1,0:T(8,128)(2,1)S(1)} all-gather(bf16[64,1008]{1,0:T(8,128)(2,1)S(1)} %start.1), channel_id=2, replica_groups=mesh['dp_0'=4,'dp_1'=8,'dp_2'=2,'mp'=8] {'mp'}, dimensions={0}, use_global_device_ids=true | all-gather | bytes 1161216 | tf_op jit(solution)/shard_map/all_gather | solution.py:317
  33.5 0.8 shard_map.67
  34.3 0.1 copy.12
  34.4 31.3 %all_to_all.44 = f32[64,1,256]{2,1,0:T(1,128)S(1)} all-to-all(f32[64,1,256]{2,1,0:T(1,128)S(1)} %copy.12), channel_id=1, replica_groups=mesh['dp_0'=4,'dp_1'=8,'dp_2'=2,'mp'=8] {'dp_0','dp_1','dp_2'}, dimensions={0} | all-to-all | bytes 131072 | tf_op jit(solution)/shard_map/all_to_all | solution.py:22
  65.8 0.1 reduce_sum.9
  65.9 0.7 broadcast_in_dim.3
  66.5 4.4 %all-to-all-start.1 = ((f32[64,1,256]{2,1,0:T(1,128)}), f32[64,1,256]{2,1,0:T(1,128)S(1)}, u32[]{:S(2)}, u32[]{:S(2)}) async-start(f32[64,1,256]{2,1,0:T(1,128)} %broadcast_in_dim.3), calls=%async_computation.1 | async-start | bytes 131072 | tf_op jit(solution)/shard_map/all_to_all | solution.py:22
  71.0 0.1 copy.13
  71.1 9.7 %all-to-all-done.1 = f32[64,1,256]{2,1,0:T(1,128)S(1)} async-done(((f32[64,1,256]{2,1,0:T(1,128)}), f32[64,1,256]{2,1,0:T(1,128)S(1)}, u32[]{:S(2)}, u32[]{:S(2)}) %all-to-all-start.1) | async-done | bytes 65568 | tf_op jit(solution)/shard_map/all_to_all | solution.py:22
  80.9 3.9 %merged.1.merged_ref = bf16[256,3968]{1,0:T(8,128)(2,1)S(1)} custom-call(bf16[256,512]{1,0:T(8,128)(2,1)S(1)} %bitcast.21, bf16[256,3968]{1,0:T(8,128)(2,1)} %e_hbm.1, bf16[3968,512]{1,0:T(8,128)(2,1)} %all-gather.3.cloned.1.call-done.x_hbm), custom_call_target="tpu_custom_call" | custom-call | flops 1040187392 | bytes 8126464 | tf_op jit(solution)/shard_map/merged/pallas_call | solution.py:125
  84.8 0.6 shard_map.68
  85.4 21.8 %all_to_all.45 = bf16[64,32,128]{2,1,0:T(8,128)(2,1)S(1)} all-to-all(bf16[64,32,128]{2,1,0:T(8,128)(2,1)S(1)} %bitcast.22), channel_id=1, replica_groups=mesh['dp_0'=4,'dp_1'=8,'dp_2'=2,'mp'=8] {'dp_0','dp_1','dp_2'}, dimensions={0} | all-to-all | bytes 1048576 | tf_op jit(solution)/shard_map/all_to_all | solution.py:22
  107.2 0.1 shard_map.69
  107.3 13.7 %all_to_all.46.second_ref = bf16[8,96,128]{2,1,0:T(8,128)(2,1)S(1)} all-to-all(bf16[8,96,128]{2,1,0:T(8,128)(2,1)S(1)} %shard_map.69), channel_id=1, replica_groups=mesh['dp_0'=4,'dp_1'=8,'dp_2'=2,'mp'=8] {'mp'}, dimensions={0} | all-to-all | bytes 393216 | tf_op jit(solution)/shard_map/all_to_all | solution.py:22
  121.1 0.9 shard_map.70
  121.9 7.4 %all-to-all-start.4 = ((bf16[64,32,128]{2,1,0:T(8,128)(2,1)}), bf16[64,32,128]{2,1,0:T(8,128)(2,1)S(1)}, u32[]{:S(2)}, u32[]{:S(2)}) async-start(bf16[64,32,128]{2,1,0:T(8,128)(2,1)} %bitcast.8), calls=%async_computation.4 | async-start | bytes 1048576 | tf_op jit(solution)/shard_map/all_to_all | solution.py:22
  129.3 3.3 %shard_map.71.inverse_ref = f32[64,64]{1,0:T(8,128)S(1)} custom-call(f32[64,64]{1,0:T(8,128)S(1)} %get-tuple-element.12.gram_ref), custom_call_target="tpu_custom_call" | custom-call | flops 1048576 | bytes 32768 | tf_op jit(solution)/shard_map/pallas_call | solution.py:40
  132.6 0.9 broadcast_multiply_fusion
  133.5 0.1 copy.14.p_ref
  133.6 13.0 %all-to-all-done.4 = bf16[64,32,128]{2,1,0:T(8,128)(2,1)S(1)} async-done(((bf16[64,32,128]{2,1,0:T(8,128)(2,1)}), bf16[64,32,128]{2,1,0:T(8,128)(2,1)S(1)}, u32[]{:S(2)}, u32[]{:S(2)}) %all-to-all-start.4) | async-done | bytes 524320 | tf_op jit(solution)/shard_map/all_to_all | solution.py:22
  146.6 3.1 %residue.1 = (bf16[256,3968]{1,0:T(8,128)(2,1)}, f32[64,496]{1,0:T(8,128)}) custom-call(s32[1]{0:T(128)} %bitcast.shard_ref, bf16[2048,128]{1,0:T(8,128)(2,1)S(1)} %bitcast.20, f32[64,64]{1,0:T(8,128)S(1)} %shard_map.71.inverse_ref, bf16[256,64]{1,0:T(8,128)(2,1)S(1)} %copy.14.p_ref, bf16[256,3968]{1,0:T(8,128)(2,1)S(1)} %merged.1.merged_ref), custom_call_target="tpu_custom_call" | custom-call | flops 130023424 | bytes 4063232 | tf_op jit(solution)/shard_map/residue/pallas_call | solution.py:287
  (7 shorter events, 0.0 us)
Async XLA Ops:
  7.2 26.4 %copy-start.1 = (bf16[512,256]{1,0:T(8,128)(2,1)S(1)}, bf16[512,256]{1,0:T(8,128)(2,1)}, u32[]{:S(2)}) copy-start(bf16[512,256]{1,0:T(8,128)(2,1)} %g_ref.1) | copy-start | bytes 786436
  7.2 26.4 %copy-start = (bf16[256,3968]{1,0:T(8,128)(2,1)S(1)}, bf16[256,3968]{1,0:T(8,128)(2,1)}, u32[]{:S(2)}) copy-start(bf16[256,3968]{1,0:T(8,128)(2,1)} %e_hbm.1) | copy-start | bytes 6094852
  7.2 73.7 %all-gather.3.cloned.1.call-start = ((), (), s32[]{:S(2)}) async-start(), calls=%async_computation.5 | async-start | bytes 4571136 | tf_op jit(solution)/shard_map/all_gather | solution.py:314
  66.5 14.3 %all-to-all-start.1 = ((f32[64,1,256]{2,1,0:T(1,128)}), f32[64,1,256]{2,1,0:T(1,128)S(1)}, u32[]{:S(2)}, u32[]{:S(2)}) async-start(f32[64,1,256]{2,1,0:T(1,128)} %broadcast_in_dim.3), calls=%async_computation.1 | async-start | bytes 131072 | tf_op jit(solution)/shard_map/all_to_all | solution.py:22
  121.9 24.7 %all-to-all-start.4 = ((bf16[64,32,128]{2,1,0:T(8,128)(2,1)}), bf16[64,32,128]{2,1,0:T(8,128)(2,1)S(1)}, u32[]{:S(2)}, u32[]{:S(2)}) async-start(bf16[64,32,128]{2,1,0:T(8,128)(2,1)} %bitcast.8), calls=%async_computation.4 | async-start | bytes 1048576 | tf_op jit(solution)/shard_map/all_to_all | solution.py:22
Sparse Core Ops, SparseCore 0:
  10.1 63.2 all-gather.2

commit v8 on v7

--- a/solution.py
+++ b/solution.py
@@ -9,6 +9,8 @@
 from jax.sharding import PartitionSpec as P
 
 DP = ("dp_0", "dp_1", "dp_2")
+CHIPS = ("dp_0", "dp_1")
+CORE = "dp_2"
 DP_MP = ("dp_0", "dp_1", "dp_2", "mp")
 BF16 = jnp.bfloat16
 F32 = jnp.float32
@@ -160,7 +162,12 @@
         spare = half + hi - end
         if spare:
             right = jnp.concatenate([right, jnp.zeros((rank, spare), F32)], axis=1)
-        out_ref[lo:hi, :] = jnp.concatenate([left, right], axis=0).T.astype(BF16)
+        out_ref[lo:hi, :] = jnp.concatenate([left, right], axis=0).T
+
+
+def pair_body(arrived_ref, out_ref):
+    near = out_ref.shape[0]
+    out_ref[...] = (arrived_ref[:near, :] + arrived_ref[near:, :]).astype(BF16)
 
 
 def spread_body(arrived_ref, gram_ref, out_ref):
@@ -250,7 +257,7 @@
         (half, jnp.concatenate([no_rows, p_rows], axis=1)),
     ]
     copies = []
-    for lo, hi in column_tiles(half):
+    for lo, hi in column_tiles(half, 1024):
         packed = packed_ref[lo:hi, :]
         q = (nn(packed, twice_high) + nn(packed, twice_low)).astype(BF16)
         for start, rows in sides:
@@ -292,7 +299,7 @@
         out_specs=[pl.BlockSpec(memory_space=pltpu.HBM), spec],
         scratch_shapes=[
             pltpu.VMEM((rows, width), BF16),
-            pltpu.SemaphoreType.DMA((2 * len(column_tiles(packed.shape[0])),)),
+            pltpu.SemaphoreType.DMA((2 * len(column_tiles(packed.shape[0], 1024)),)),
         ],
         compiler_params=pltpu.CompilerParams(vmem_limit_bytes=GRANT),
         cost_estimate=pl.CostEstimate(
@@ -330,23 +337,25 @@
     near = -(-width // (2 * replicas * 16)) * 16
     product, gram_part = local_call(
         product_body,
-        [shaped((replicas * near, 2 * rank), BF16), shaped((rank, rank), F32)],
+        [shaped((replicas * near, 2 * rank), F32), shaped((rank, rank), F32)],
         p_t,
         merged,
         flops=2 * rows * width * rank,
     )
+    own = replicas * near // lax.axis_size(CORE)
+    (summed,) = local_call(pair_body, [shaped((own, 2 * rank), BF16)], exchange(product, CORE))
     (pieces,) = local_call(
         spread_body,
         [shaped((shards, rank + near, 2 * rank), BF16)],
-        exchange(product, DP),
+        exchange(summed, CHIPS),
         gram_part,
     )
     q_copies, gram = local_call(
         functools.partial(settle_body, replicas=replicas),
-        [shaped(product.shape, BF16), shaped((rank, rank), F32)],
+        [shaped(summed.shape, BF16), shaped((rank, rank), F32)],
         exchange(pieces, "mp"),
     )
-    packed = exchange(q_copies, DP)
+    packed = sent_to_all(exchange(q_copies, CHIPS), CORE).reshape(product.shape)
     (inverse,) = local_call(inverse_body, [shaped((rank, rank), F32)], gram, flops=4 * rank**3)
     p_hat = nn(inverse, p_t, precision=HIGHEST)
     shard = lax.axis_index("mp").astype(jnp.int32).reshape(1)

time: 157 us -> 152 us (0.968)
  waiting for transfers between devices: 23.4 us -> 15.8 us
  blocking collectives: 91.1 us -> 94.4 us
    all_to_all x2, waiting for transfers between devices: 22.7 us -> 15.1 us  [exchange(): return lax.all_to_all(pieces, axes, split_axis=0, concat_axis=0, tiled=True)]
    all_to_all x3 -> x5, blocking collectives: 66.9 us -> 70.2 us  [exchange(): return lax.all_to_all(pieces, axes, split_axis=0, concat_axis=0, tiled=True)]
    pallas_call x5 -> x6, Pallas kernels: 5.64 us -> 5.57 us  [local_call(): pl.pallas_call(body, out_shape=list(outs), in_specs=[spec] * len(args), o...]
  transfers between devices with their start and end apart: 3 -> 3, of which waited for: 2 -> 2; matrix products, arithmetic and copies ran while one was open for 1% -> 1% of each run, Pallas kernels for 3% -> 4%
where the time goes in v8:
time: 152 us
  blocking collectives  94.4 us (62%)
  waiting for transfers between devices  15.8 us (10%)
  between operations  14.1 us (9%)
  Pallas kernels  13.9 us (9%)
  starting transfers between devices  11.3 us (7%)
    all_to_all x5, blocking collectives, exchange(): return lax.all_to_all(pieces, axes, split_axis=0, concat_axis=0, tiled=True)  70.2 us
    all_gather x1, blocking collectives, layer(): first = lax.all_gather(sent, 'mp')  24.2 us
    all_to_all x2, waiting for transfers between devices, exchange(): return lax.all_to_all(pieces, axes, split_axis=0, concat_axis=0, tiled=True)  15.1 us
    all_to_all x2, starting transfers between devices, exchange(): return lax.all_to_all(pieces, axes, split_axis=0, concat_axis=0, tiled=True)  11.2 us
    pallas_call x6, Pallas kernels, local_call(): pl.pallas_call(body, out_shape=list(outs), in_specs=[spec] * len(args), o...  5.57 us
    pallas_call x1, Pallas kernels, merge(): pl.pallas_call(merged_body, name='merged', out_shape=shaped((rows, width)...  3.94 us
  transfers between devices with their start and end apart: 3, of which 2 were waited for; matrix products, arithmetic and copies ran while one was open for 1% of the time, Pallas kernels for 4%

profile of v8, /device:TPU:1, one launch (start us, length us, event | category | flops | bytes accessed | tf_op | source)
XLA Modules:
  0.0 151.5 jit_solution(1171656787951129060)
XLA Ops:
  7.2 0.7 all-gather.3.cloned.1.call-update
  7.9 1.4 start.1
  9.3 24.2 %all-gather = bf16[512,1008]{1,0:T(8,128)(2,1)S(1)} all-gather(bf16[64,1008]{1,0:T(8,128)(2,1)S(1)} %start.1), channel_id=2, replica_groups=mesh['dp_0'=4,'dp_1'=8,'dp_2'=2,'mp'=8] {'mp'}, dimensions={0}, use_global_device_ids=true | all-gather | bytes 1161216 | tf_op jit(solution)/shard_map/all_gather | solution.py:324
  33.5 0.8 shard_map.67
  34.4 31.3 %all_to_all.61 = f32[64,1,256]{2,1,0:T(1,128)S(1)} all-to-all(f32[64,1,256]{2,1,0:T(1,128)S(1)} %copy.12), channel_id=1, replica_groups=mesh['dp_0'=4,'dp_1'=8,'dp_2'=2,'mp'=8] {'dp_0','dp_1','dp_2'}, dimensions={0} | all-to-all | bytes 131072 | tf_op jit(solution)/shard_map/all_to_all | solution.py:24
  65.8 0.1 reduce_sum.9
  65.9 0.7 broadcast_in_dim.6
  66.5 4.4 %all-to-all-start.1 = ((f32[64,1,256]{2,1,0:T(1,128)}), f32[64,1,256]{2,1,0:T(1,128)S(1)}, u32[]{:S(2)}, u32[]{:S(2)}) async-start(f32[64,1,256]{2,1,0:T(1,128)} %broadcast_in_dim.6), calls=%async_computation.1 | async-start | bytes 131072 | tf_op jit(solution)/shard_map/all_to_all | solution.py:24
  71.0 0.1 copy.13
  71.1 9.7 %all-to-all-done.1 = f32[64,1,256]{2,1,0:T(1,128)S(1)} async-done(((f32[64,1,256]{2,1,0:T(1,128)}), f32[64,1,256]{2,1,0:T(1,128)S(1)}, u32[]{:S(2)}, u32[]{:S(2)}) %all-to-all-start.1) | async-done | bytes 65568 | tf_op jit(solution)/shard_map/all_to_all | solution.py:24
  80.9 3.9 %merged.1.merged_ref = bf16[256,3968]{1,0:T(8,128)(2,1)S(1)} custom-call(bf16[256,512]{1,0:T(8,128)(2,1)S(1)} %bitcast.24, bf16[256,3968]{1,0:T(8,128)(2,1)} %e_hbm.1, bf16[3968,512]{1,0:T(8,128)(2,1)} %all-gather.3.cloned.1.call-done.x_hbm), custom_call_target="tpu_custom_call" | custom-call | flops 1040187392 | bytes 8126464 | tf_op jit(solution)/shard_map/merged/pallas_call | solution.py:127
  84.8 0.6 shard_map.68
  85.4 4.6 %all_to_all.62 = f32[2,1024,128]{2,1,0:T(8,128)S(1)} all-to-all(f32[2,1024,128]{2,1,0:T(8,128)S(1)} %bitcast.26), channel_id=1, replica_groups=mesh['dp_0'=4,'dp_1'=8,'dp_2'=2,'mp'=8] {'dp_2'}, dimensions={0} | all-to-all | bytes 2097152 | tf_op jit(solution)/shard_map/all_to_all | solution.py:24
  90.1 13.3 %all_to_all.63 = bf16[32,32,128]{2,1,0:T(8,128)(2,1)S(1)} all-to-all(bf16[32,32,128]{2,1,0:T(8,128)(2,1)S(1)} %bitcast.25), channel_id=1, replica_groups=mesh['dp_0'=4,'dp_1'=8,'dp_2'=2,'mp'=8] {'dp_0','dp_1'}, dimensions={0} | all-to-all | bytes 524288 | tf_op jit(solution)/shard_map/all_to_all | solution.py:24
  103.4 0.1 shard_map.70
  103.5 12.8 %all_to_all.64.second_ref = bf16[8,96,128]{2,1,0:T(8,128)(2,1)S(1)} all-to-all(bf16[8,96,128]{2,1,0:T(8,128)(2,1)S(1)} %shard_map.70), channel_id=1, replica_groups=mesh['dp_0'=4,'dp_1'=8,'dp_2'=2,'mp'=8] {'mp'}, dimensions={0} | all-to-all | bytes 393216 | tf_op jit(solution)/shard_map/all_to_all | solution.py:24
  116.3 0.7 shard_map.71
  117.1 6.8 %all-to-all-start.5 = ((bf16[32,32,128]{2,1,0:T(8,128)(2,1)}), bf16[32,32,128]{2,1,0:T(8,128)(2,1)S(1)}, u32[]{:S(2)}, u32[]{:S(2)}) async-start(bf16[32,32,128]{2,1,0:T(8,128)(2,1)} %bitcast.10), calls=%async_computation.5 | async-start | bytes 524288 | tf_op jit(solution)/shard_map/all_to_all | solution.py:24
  123.9 3.3 %shard_map.72.inverse_ref = f32[64,64]{1,0:T(8,128)S(1)} custom-call(f32[64,64]{1,0:T(8,128)S(1)} %get-tuple-element.12.gram_ref), custom_call_target="tpu_custom_call" | custom-call | flops 1048576 | bytes 32768 | tf_op jit(solution)/shard_map/pallas_call | solution.py:42
  127.2 0.9 broadcast_multiply_fusion
  128.1 0.1 copy.14.p_ref
  128.2 5.4 %all-to-all-done.5 = bf16[32,32,128]{2,1,0:T(8,128)(2,1)S(1)} async-done(((bf16[32,32,128]{2,1,0:T(8,128)(2,1)}), bf16[32,32,128]{2,1,0:T(8,128)(2,1)S(1)}, u32[]{:S(2)}, u32[]{:S(2)}) %all-to-all-start.5) | async-done | bytes 262176 | tf_op jit(solution)/shard_map/all_to_all | solution.py:24
  133.6 8.1 %all_to_all.65 = bf16[2,1024,128]{2,1,0:T(8,128)(2,1)S(1)} all-to-all(bf16[2,1024,128]{2,1,0:T(8,128)(2,1)S(1)} %broadcast_in_dim.7), channel_id=1, replica_groups=mesh['dp_0'=4,'dp_1'=8,'dp_2'=2,'mp'=8] {'dp_2'}, dimensions={0} | all-to-all | bytes 1048576 | tf_op jit(solution)/shard_map/all_to_all | solution.py:24
  141.7 3.0 %residue.1 = (bf16[256,3968]{1,0:T(8,128)(2,1)}, f32[64,496]{1,0:T(8,128)}) custom-call(s32[1]{0:T(128)} %bitcast.shard_ref, bf16[2048,128]{1,0:T(8,128)(2,1)S(1)} %bitcast.23, f32[64,64]{1,0:T(8,128)S(1)} %shard_map.72.inverse_ref, bf16[256,64]{1,0:T(8,128)(2,1)S(1)} %copy.14.p_ref, bf16[256,3968]{1,0:T(8,128)(2,1)S(1)} %merged.1.merged_ref), custom_call_target="tpu_custom_call" | custom-call | flops 130023424 | bytes 4063232 | tf_op jit(solution)/shard_map/residue/pallas_call | solution.py:294
  (11 shorter events, 0.2 us)
Async XLA Ops:
  7.2 26.4 %copy-start.1 = (bf16[512,256]{1,0:T(8,128)(2,1)S(1)}, bf16[512,256]{1,0:T(8,128)(2,1)}, u32[]{:S(2)}) copy-start(bf16[512,256]{1,0:T(8,128)(2,1)} %g_ref.1) | copy-start | bytes 786436
  7.2 26.4 %copy-start = (bf16[256,3968]{1,0:T(8,128)(2,1)S(1)}, bf16[256,3968]{1,0:T(8,128)(2,1)}, u32[]{:S(2)}) copy-start(bf16[256,3968]{1,0:T(8,128)(2,1)} %e_hbm.1) | copy-start | bytes 6094852
  7.2 73.7 %all-gather.3.cloned.1.call-start = ((), (), s32[]{:S(2)}) async-start(), calls=%async_computation.7 | async-start | bytes 4571136 | tf_op jit(solution)/shard_map/all_gather | solution.py:321
  66.5 14.3 %all-to-all-start.1 = ((f32[64,1,256]{2,1,0:T(1,128)}), f32[64,1,256]{2,1,0:T(1,128)S(1)}, u32[]{:S(2)}, u32[]{:S(2)}) async-start(f32[64,1,256]{2,1,0:T(1,128)} %broadcast_in_dim.6), calls=%async_computation.1 | async-start | bytes 131072 | tf_op jit(solution)/shard_map/all_to_all | solution.py:24
  117.1 16.5 %all-to-all-start.5 = ((bf16[32,32,128]{2,1,0:T(8,128)(2,1)}), bf16[32,32,128]{2,1,0:T(8,128)(2,1)S(1)}, u32[]{:S(2)}, u32[]{:S(2)}) async-start(bf16[32,32,128]{2,1,0:T(8,128)(2,1)} %bitcast.10), calls=%async_computation.5 | async-start | bytes 524288 | tf_op jit(solution)/shard_map/all_to_all | solution.py:24
Sparse Core Ops, SparseCore 0:
  10.1 63.2 all-gather.2
